TPU v7x, 128 devices: a whole 4x4x4 slice. The times are simulated.
128 devices in a mesh: rows: 32 (over z, y, core), vecs: 4 (over x).
Axes of the slice: x: 4, y: 4, z: 4, core: 2. Of those that a mesh axis runs over, the one named last changes fastest.
Arguments:
- basis: bfloat16 [100, 2097152], P('vecs', 'rows'), may hold values from -6 to 6
- coefficients: bfloat16 [100, 40], replicated, may hold values from -0.625 to 0.625
- eigen_values: float32 [40], P('vecs'), may hold values from -3 to 1
- stiffness: float32 [2097152], P('rows'), may hold values from 6.5 to 10
- damping: float32 [2097152], P('rows'), may hold values from 0.2 to 2
- mass: float32 [2097152], P('rows'), may hold values from 0.5 to 2
- link_count: int32 [32], P('rows'), may hold values from 1024 to 4096, as said below
- lower_cells: int32 [32, 4096], P('rows'), may hold values from 0 to 4095
- upper_cells: int32 [32, 4096], P('rows'), may hold values from 0 to 4095
Outputs:
- eigvecs: bfloat16 [40, 2097152], P('vecs', 'rows')
- residuals: bfloat16 [40, 2097152], P('vecs', 'rows')
- relative_norms: float32 [40], P('vecs')
Inputs may be any that keep to these rules, and one draw needn't show every extreme that they name: Interface s joins subdomain s to subdomain (s + 1) mod 32; only its first link_count[s] slots are used, the others are to be ignored. Some interface uses all 4096 slots in every draw. `lower_cells`: slots beyond link_count[s] hold values that are not used. `upper_cells`: slots beyond link_count[s] hold values that are not used.
All inputs are finite; a program needn't handle non-finite values.
Results may differ from a plain program's by a relative error of at most 0.0037.
The roundings to bfloat16 on the way count: a program that leaves them out, or rounds other values in their place, can miss the bound.
Values may be sent and summed in bfloat16 or wider, within the bound.
A program may use at most 320 MiB of HBM per device.

v0:
```python
import functools

import jax
import jax.numpy as jnp
from jax import lax
from jax.experimental import pallas as pl
from jax.experimental.pallas import tpu as pltpu
from jax.sharding import PartitionSpec as P

WID = 64
LANES = 128
PAD = 16
BLOCK = 512
FULL = 8


def remote(src, dst, send_sem, recv_sem, where):
    return pltpu.make_async_remote_copy(
        src_ref=src,
        dst_ref=dst,
        send_sem=send_sem,
        recv_sem=recv_sem,
        device_id=where,
        device_id_type=pl.DeviceIdType.MESH,
    )


def kernel(
    count,
    planes,
    cells,
    vector_part,
    basis,
    coefficients_in,
    eigen_in,
    stiffness_in,
    damping_in,
    mass_in,
    used_in,
    lower_in,
    upper_in,
    eig_out,
    res_out,
    norm_out,
    own_basis,
    mate_basis,
    wire_out,
    wire_in,
    values,
    face_out,
    face_in,
    links_in,
    link_sums,
    link_part,
    stat_out,
    stat_in,
    links,
    factors,
    stiffness,
    damping,
    mass,
    stat_line,
    coefficients,
    eigen,
    used,
    lower,
    upper,
    input_sem,
    local_sem,
    mate_send,
    mate_recv,
    wire_send,
    wire_recv,
    face_send,
    face_recv,
    stat_send,
    stat_recv,
):
    row = lax.axis_index("rows")
    vec = lax.axis_index("vecs")
    mate = {"vecs": vec + 1 - 2 * (vec % 2)}
    across = {"vecs": (vec + 2) % 4}
    above = {"rows": (row + 1) % count}
    below = {"rows": (row + count - 1) % count}
    half = cells // 2
    eighth = cells // 8
    slots = links.shape[1]
    rank_part = basis.shape[0]

    def plane_at(step):
        return (step + planes - 1) % planes

    def lanes_of(plane):
        return pl.ds(pl.multiple_of(plane * cells, cells), cells)

    def local_copy(plane):
        return pltpu.make_async_copy(
            basis.at[:, lanes_of(plane)], own_basis.at[:, lanes_of(plane)], local_sem.at[plane]
        )

    def mate_copy(plane):
        return remote(
            own_basis.at[:, lanes_of(plane)],
            mate_basis.at[:, lanes_of(plane)],
            mate_send.at[plane],
            mate_recv.at[plane],
            mate,
        )

    def wire_copy(plane):
        return remote(
            wire_out.at[plane], wire_in.at[plane], wire_send.at[plane], wire_recv.at[plane], across
        )

    def face_copy(which):
        return remote(
            face_out.at[which],
            face_in.at[which],
            face_send.at[which],
            face_recv.at[which],
            above if which == 0 else below,
        )

    def links_copy():
        return remote(links, links_in, face_send.at[2], face_recv.at[2], above)

    def stat_copy(step):
        return remote(
            stat_line,
            stat_in.at[step],
            stat_send.at[step],
            stat_recv.at[step],
            {"rows": (row + step) % count},
        )

    def each(first, last, body):
        def run(step, carry):
            body(step)
            return carry

        lax.fori_loop(first, last, run, 0)

    barrier = pltpu.get_barrier_semaphore()

    def greet(where):
        pl.semaphore_signal(barrier, inc=1, device_id=where, device_id_type=pl.DeviceIdType.MESH)

    each(1, count, lambda step: greet({"rows": (row + step) % count}))
    greet(mate)
    greet(across)

    inputs = [
        pltpu.make_async_copy(source, target, input_sem.at[place])
        for place, (source, target) in enumerate(
            (
                (coefficients_in, coefficients),
                (eigen_in, eigen),
                (used_in, used),
                (lower_in, lower),
                (upper_in, upper),
                (stiffness_in, stiffness),
                (damping_in, damping),
                (mass_in, mass),
            )
        )
    ]
    for copy in inputs[:5]:
        copy.start()
    each(0, planes, lambda step: local_copy(plane_at(step)).start())
    for copy in inputs[5:]:
        copy.start()

    values[...] = jnp.zeros_like(values)
    stat_out[...] = jnp.zeros_like(stat_out)
    for copy in inputs[:5]:
        copy.wait()

    slot = lax.broadcasted_iota(jnp.int32, (1, slots), 1)
    is_used = slot < used[0]
    links[...] = jnp.full_like(links, -1)
    links[0:1] = jnp.where(is_used, lower[...], -1)
    links[1:2] = jnp.where(is_used, upper[...], -1)

    total_vectors, total_rank = coefficients.shape
    place = lax.broadcasted_iota(jnp.int32, (2 * PAD, total_vectors), 0)
    vector = lax.broadcasted_iota(jnp.int32, (2 * PAD, total_vectors), 1)
    owner = jnp.where(place < PAD, vec, (vec + 2) % 4)
    inside = place % PAD
    choose = (inside < vector_part) & (vector == owner * vector_part + inside)
    choose = jnp.where(choose, 1.0, 0.0).astype(jnp.bfloat16)
    chosen = jnp.dot(choose, coefficients[...], preferred_element_type=jnp.float32)
    chosen = chosen.astype(jnp.bfloat16)
    rank = lax.broadcasted_iota(jnp.int32, (total_rank, rank_part), 0)
    own_rank = lax.broadcasted_iota(jnp.int32, (total_rank, rank_part), 1)
    for side, source in enumerate((vec, vec + 1 - 2 * (vec % 2))):
        pick = jnp.where(rank == source * rank_part + own_rank, 1.0, 0.0).astype(jnp.bfloat16)
        part = jnp.dot(chosen, pick, preferred_element_type=jnp.float32)
        factors[side] = part.astype(jnp.bfloat16)

    pl.semaphore_wait(barrier, count + 1)

    def pass_on(step):
        local_copy(plane_at(step)).wait()
        mate_copy(plane_at(step)).start()

    each(0, planes, pass_on)
    links_copy().start()

    row_iota = lax.broadcasted_iota(jnp.int32, (FULL, eighth), 0)
    rest = row_iota < vector_part - FULL

    def produce(step):
        plane = plane_at(step)
        mate_copy(plane).wait_recv()
        both = jnp.dot(
            factors[0], own_basis[:, lanes_of(plane)], preferred_element_type=jnp.float32
        ) + jnp.dot(factors[1], mate_basis[:, lanes_of(plane)], preferred_element_type=jnp.float32)
        values[plane + 1, :, LANES : LANES + cells] = both[:PAD]
        top = both[PAD : PAD + FULL]
        tail = both[PAD + FULL :]
        wire_out[plane, :, :half] = jnp.concatenate([top[:, :half], top[:, half:]], axis=0).astype(
            jnp.bfloat16
        )
        packed = []
        for side in range(2):
            total = None
            for part in range(4):
                start = (4 * side + part) * eighth
                piece = tail[:, start : start + eighth]
                if part:
                    piece = pltpu.roll(piece, 2 * part, 0)
                total = piece if total is None else total + piece
            packed.append(total)
        wire_out[plane, :, half:] = jnp.concatenate(packed, axis=0).astype(jnp.bfloat16)
        wire_copy(plane).start()

    each(0, planes, produce)
    for copy in inputs[5:]:
        copy.wait()

    def fold(block):
        total = block[:, :LANES]
        for start in range(LANES, block.shape[1], LANES):
            total = total + block[:, start : start + LANES]
        return total

    def finish(plane):
        wire_copy(plane).wait_recv()
        squares = jnp.zeros((PAD, LANES), jnp.float32)
        for part in range(8):
            side = part // 4
            lanes = slice(LANES + part * eighth, LANES + (part + 1) * eighth)
            inner = (part % 4) * eighth
            top = wire_in[plane, :, inner : inner + eighth].astype(jnp.float32)
            top = top[side * FULL : (side + 1) * FULL]
            tail = wire_in[plane, :, half:].astype(jnp.float32)
            tail = tail[side * FULL : (side + 1) * FULL]
            if part % 4:
                tail = pltpu.roll(tail, FULL - 2 * (part % 4), 0)
            tail = jnp.where(rest, tail, 0.0)
            held = values[plane + 1, :, lanes] + jnp.concatenate([top, tail], axis=0)
            rounded = held.astype(jnp.bfloat16)
            exact = rounded.astype(jnp.float32)
            values[plane + 1, :, lanes] = exact
            start = pl.multiple_of(plane * cells + part * eighth, eighth)
            eig_out[:, pl.ds(start, eighth)] = rounded[:vector_part]
            squares = squares + fold(exact * exact)
        stat_out[:PAD] += squares

    diag = lax.broadcasted_iota(jnp.int32, (PAD, vector_part), 0) == lax.broadcasted_iota(
        jnp.int32, (PAD, vector_part), 1
    )
    lam = jnp.where(diag, jnp.broadcast_to(eigen[...], (PAD, vector_part)), 0.0)
    lam = jnp.sum(lam, axis=1, keepdims=True)
    lam_b = jnp.broadcast_to(lam, (PAD, LANES))
    lam_sq = jnp.tile(lam_b * lam_b, (1, BLOCK // LANES))
    lam_b = jnp.tile(lam_b, (1, BLOCK // LANES))
    coupling = lam_sq * 0.1 + lam_b * 0.3 + 1.0
    column = lax.broadcasted_iota(jnp.int32, (PAD, BLOCK), 1) % WID
    wide = BLOCK + 2 * LANES

    def stencil(plane, link):
        squares = jnp.zeros((PAD, LANES), jnp.float32)
        for start in range(0, cells, BLOCK):
            inner = slice(LANES + start, LANES + start + BLOCK)
            around = values[plane + 1, :, start : start + wide]
            mid = around[:, LANES : LANES + BLOCK]

            def moved(amount):
                return pltpu.roll(around, amount % wide, 1)[:, LANES : LANES + BLOCK]

            total = values[plane, :, inner] + values[plane + 2, :, inner]
            total = total + (moved(WID) + moved(-WID))
            total = total + jnp.where(column < WID - 1, moved(-1), 0.0)
            total = total + jnp.where(column > 0, moved(1), 0.0)
            if link is not None:
                total = total + link_sums[link, :, start : start + BLOCK]
            at = pl.ds(pl.multiple_of(plane * cells + start, BLOCK), BLOCK)
            diagonal = lam_sq * mass[:, at] + lam_b * damping[:, at] + stiffness[:, at]
            full = diagonal * mid - coupling * total
            res_out[:, at] = full.astype(jnp.bfloat16)[:vector_part]
            squares = squares + fold(full * full)
        stat_out[PAD:] += squares

    tiles = cells // LANES

    def link_side(which, lists, source_row, target_row):
        stacked = jnp.concatenate(
            [face_in[which, :, t * LANES : (t + 1) * LANES] for t in range(tiles)], axis=0
        )
        link_part[...] = jnp.zeros_like(link_part)
        low_iota = lax.broadcasted_iota(jnp.int32, (LANES, BLOCK), 0)

        def some(step):
            at = pl.ds(pl.multiple_of(step * BLOCK, BLOCK), BLOCK)
            source = lists[source_row : source_row + 1, at]
            target = lists[target_row : target_row + 1, at]
            low = jnp.where(low_iota == (source & (LANES - 1)), 1.0, 0.0).astype(jnp.bfloat16)
            picked = jnp.dot(stacked, low, preferred_element_type=jnp.float32)
            high = jnp.broadcast_to(source >> 7, (PAD, BLOCK))
            got = jnp.zeros((PAD, BLOCK), jnp.float32)
            for t in range(tiles):
                got = got + jnp.where(high == t, picked[t * PAD : (t + 1) * PAD], 0.0)
            high = jnp.broadcast_to(target >> 7, (PAD, BLOCK))
            spread = jnp.concatenate(
                [jnp.where(high == t, got, 0.0).astype(jnp.bfloat16) for t in range(tiles)], axis=0
            )
            low = jnp.where(low_iota == (target & (LANES - 1)), 1.0, 0.0).astype(jnp.bfloat16)
            link_part[...] += lax.dot_general(
                spread, low, (((1,), (1,)), ((), ())), preferred_element_type=jnp.float32
            )

        each(0, slots // BLOCK, some)
        for t in range(tiles):
            link_sums[which, :, t * LANES : (t + 1) * LANES] = link_part[t * PAD : (t + 1) * PAD]

    def send_face(which, plane):
        face_out[which] = values[plane + 1, :, LANES : LANES + cells].astype(jnp.bfloat16)
        face_copy(which).start()

    finish(planes - 1)
    send_face(0, planes - 1)
    finish(0)
    send_face(1, 0)
    finish(1)

    def advance(plane):
        finish(plane)
        stencil(plane - 1, None)

    middle = min(4, planes - 1)
    each(2, middle, advance)
    face_copy(0).wait_recv()
    links_copy().wait_recv()
    link_side(0, links_in, 0, 1)
    face_copy(1).wait_recv()
    link_side(1, links, 1, 0)
    stencil(0, 0)
    each(middle, planes - 1, advance)
    stencil(planes - 2, None)
    stencil(planes - 1, 1)

    sums = jnp.sum(stat_out[...], axis=1, keepdims=True)
    spot = lax.broadcasted_iota(jnp.int32, (2 * PAD, LANES), 0) == lax.broadcasted_iota(
        jnp.int32, (2 * PAD, LANES), 1
    )
    line = jnp.sum(jnp.where(spot, sums, 0.0), axis=0, keepdims=True)
    stat_line[...] = line
    each(1, count, lambda step: stat_copy(step).start())
    each(0, planes, lambda plane: mate_copy(plane).wait_send())
    each(0, planes, lambda plane: wire_copy(plane).wait_send())
    links_copy().wait_send()
    face_copy(0).wait_send()
    face_copy(1).wait_send()
    each(1, count, lambda step: stat_copy(step).wait_recv())
    for step in range(1, count):
        line = line + stat_in[step]
    norms = jnp.sqrt(line[:, PAD : PAD + vector_part]) / jnp.sqrt(line[:, :vector_part] + 1.0)
    norm_out[...] = norms
    each(1, count, lambda step: stat_copy(step).wait_send())


def write_back(eig_held, res_held, norm_held, eig_out, res_out, norm_out, sem):
    copies = [
        pltpu.make_async_copy(source, target, sem.at[place])
        for place, (source, target) in enumerate(
            ((eig_held, eig_out), (res_held, res_out), (norm_held, norm_out))
        )
    ]
    for copy in copies:
        copy.start()
    for copy in copies:
        copy.wait()


def on_device(
    basis,
    coefficients,
    eigen_values,
    stiffness,
    damping,
    mass,
    link_count,
    lower_cells,
    upper_cells,
):
    count = lax.axis_size("rows")
    vector_part = eigen_values.shape[0]
    rank_part, rows_local = basis.shape
    cells = WID * WID
    planes = rows_local // cells
    slots = lower_cells.shape[1]
    vmem = pl.BlockSpec(memory_space=pltpu.VMEM)
    anywhere = pl.BlockSpec(memory_space=pltpu.HBM)
    wire = cells // 2 + cells // 8
    dma = pltpu.SemaphoreType.DMA
    eigvecs, residuals, norms = pl.pallas_call(
        functools.partial(kernel, count, planes, cells, vector_part),
        out_shape=(
            pltpu.VMEM((vector_part, rows_local), jnp.bfloat16),
            pltpu.VMEM((vector_part, rows_local), jnp.bfloat16),
            pltpu.VMEM((1, vector_part), jnp.float32),
        ),
        in_specs=[anywhere] * 9,
        out_specs=(vmem, vmem, vmem),
        scratch_shapes=[
            pltpu.VMEM((rank_part, rows_local), jnp.bfloat16),
            pltpu.VMEM((rank_part, rows_local), jnp.bfloat16),
            pltpu.VMEM((planes, PAD, wire), jnp.bfloat16),
            pltpu.VMEM((planes, PAD, wire), jnp.bfloat16),
            pltpu.VMEM((planes + 2, PAD, cells + 2 * LANES), jnp.float32),
            pltpu.VMEM((2, PAD, cells), jnp.bfloat16),
            pltpu.VMEM((2, PAD, cells), jnp.bfloat16),
            pltpu.VMEM((8, slots), jnp.int32),
            pltpu.VMEM((2, PAD, cells), jnp.float32),
            pltpu.VMEM((cells // LANES * PAD, LANES), jnp.float32),
            pltpu.VMEM((2 * PAD, LANES), jnp.float32),
            pltpu.VMEM((count, 1, LANES), jnp.float32),
            pltpu.VMEM((8, slots), jnp.int32),
            pltpu.VMEM((2, 2 * PAD, rank_part), jnp.bfloat16),
            pltpu.VMEM((1, rows_local), jnp.float32),
            pltpu.VMEM((1, rows_local), jnp.float32),
            pltpu.VMEM((1, rows_local), jnp.float32),
            pltpu.VMEM((1, LANES), jnp.float32),
            pltpu.VMEM(coefficients.shape[::-1], jnp.bfloat16),
            pltpu.VMEM((1, vector_part), jnp.float32),
            pltpu.SMEM((1,), jnp.int32),
            pltpu.VMEM((1, slots), jnp.int32),
            pltpu.VMEM((1, slots), jnp.int32),
            dma((8,)),
            dma((planes,)),
            dma((planes,)),
            dma((planes,)),
            dma((planes,)),
            dma((planes,)),
            dma((3,)),
            dma((3,)),
            dma((count,)),
            dma((count,)),
        ],
        compiler_params=pltpu.CompilerParams(
            collective_id=0, has_side_effects=True, vmem_limit_bytes=56 * 1024 * 1024
        ),
    )(
        basis,
        coefficients.T,
        eigen_values[None, :],
        stiffness[None, :],
        damping[None, :],
        mass[None, :],
        link_count,
        lower_cells,
        upper_cells,
    )
    eigvecs, residuals, norms = pl.pallas_call(
        write_back,
        out_shape=tuple(
            jax.ShapeDtypeStruct(held.shape, held.dtype) for held in (eigvecs, residuals, norms)
        ),
        in_specs=[vmem] * 3,
        out_specs=[pl.BlockSpec(memory_space=pl.ANY)] * 3,
        scratch_shapes=[dma((3,))],
        compiler_params=pltpu.CompilerParams(vmem_limit_bytes=1 << 20),
    )(eigvecs, residuals, norms)
    return eigvecs, residuals, norms[0]


def solution(mesh):
    placed = (
        P("vecs", "rows"),
        P(),
        P("vecs"),
        P("rows"),
        P("rows"),
        P("rows"),
        P("rows"),
        P("rows", None),
        P("rows", None),
    )
    return jax.shard_map(
        on_device,
        mesh=mesh,
        in_specs=placed,
        out_specs=(P("vecs", "rows"), P("vecs", "rows"), P("vecs")),
        check_vma=False,
    )
```

profile of v0, /device:TPU:1, one launch (start us, length us, event | category | flops | bytes accessed | tf_op | source)
XLA Modules:
  0.0 140.0 jit_solution(16993644263652397669)
XLA Ops:
  1.3 136.7 %shard_map.112 = (bf16[10,65536]{1,0:T(8,128)(2,1)S(1)}, bf16[10,65536]{1,0:T(8,128)(2,1)S(1)}, f32[1,10]{1,0:T(1,128)S(1)}) custom-call(bf16[25,65536]{1,0:T(8,128)(2,1)} %basis.1, bf16[40,100]{1,0:T(8,128)(2,1)} %bitcast.9, f32[1,10]{1,0:T(1,128)} %bitcast.10, f32[1,65536]{1,0:T(1,128)} %bitcast.6, f32[1,65536]{1,0:T(1,128)} %bitcast.7, ...), custom_call_target="tpu_custom_call" | custom-call | tf_op jit(solution)/shard_map/pallas_call | solution.py:417
  138.0 2.0 %shard_map.113 = (bf16[10,65536]{1,0:T(8,128)(2,1)}, bf16[10,65536]{1,0:T(8,128)(2,1)}, f32[1,10]{1,0:T(1,128)}) custom-call(bf16[10,65536]{1,0:T(8,128)(2,1)S(1)} %get-tuple-element.9.eig_held, bf16[10,65536]{1,0:T(8,128)(2,1)S(1)} %get-tuple-element.10.res_held, f32[1,10]{1,0:T(1,128)S(1)} %get-tuple-element.11.norm_held), custom_call_target="tpu_custom_call" | custom-call | tf_op jit(solution)/shard_map/pallas_call | solution.py:475
where the time goes:
time: 140 us
  Pallas kernels  139 us (99%)
    pallas_call x1, Pallas kernels, on_device(): pl.pallas_call(functools.partial(kernel, count, planes, cells, vector_par...  137 us

commit v1 on v0

v1 whole, which is shorter than its diff:
```python
import functools

import jax
import jax.numpy as jnp
from jax import lax
from jax.experimental import pallas as pl
from jax.experimental.pallas import tpu as pltpu
from jax.sharding import PartitionSpec as P

WID = 64
LANES = 128
CHUNKS = 8
DEPTH = 32
PAD = 16
BLOCK = 512
LEAD = 6
LAG = 2
LINKS_AT = 7


def remote(src, dst, send_sem, recv_sem, where):
    return pltpu.make_async_remote_copy(
        src_ref=src,
        dst_ref=dst,
        send_sem=send_sem,
        recv_sem=recv_sem,
        device_id=where,
        device_id_type=pl.DeviceIdType.MESH,
    )


def iota(shape, axis):
    return lax.broadcasted_iota(jnp.int32, shape, axis)


def ones_where(condition):
    return jnp.where(condition, 1.0, 0.0).astype(jnp.bfloat16)


def kernel(
    count,
    planes,
    cells,
    vector_part,
    rank_part,
    basis,
    coefficients_in,
    eigen_in,
    stiffness_in,
    damping_in,
    mass_in,
    used_in,
    lower_in,
    upper_in,
    eig_out,
    res_out,
    norm_out,
    own_basis,
    first_out,
    first_in,
    along_out,
    along_in,
    back_out,
    back_in,
    middle,
    values,
    packed,
    res_packed,
    face_in,
    links_in,
    links,
    link_sums,
    stat_out,
    stat_in,
    stat_line,
    factors,
    spread_rows,
    chunk_ones,
    lam_of,
    stiffness,
    damping,
    mass,
    coefficients,
    eigen,
    used,
    lower,
    upper,
    input_sem,
    local_sem,
    first_send,
    first_recv,
    along_send,
    along_recv,
    back_send,
    back_recv,
    face_send,
    face_recv,
    stat_send,
    stat_recv,
):
    row = lax.axis_index("rows")
    vec = lax.axis_index("vecs")
    vecs = 4
    above = {"rows": (row + 1) % count}
    below = {"rows": (row + count - 1) % count}
    slots = links.shape[1] // 2
    width = cells // CHUNKS
    parts = width // LANES
    held = vector_part * CHUNKS
    plane_rows = cells // LANES

    def plane_at(step):
        return (step + planes - 1) % planes

    def toward(step):
        return {"vecs": (vec + 1 + 2 * (step % 2)) % vecs}

    def away(step):
        return {"vecs": (vec + 3 - 2 * (step % 2)) % vecs}

    def local_copy(step):
        start = pl.multiple_of(plane_at(step) * cells, cells)
        return pltpu.make_async_copy(
            basis.at[:, pl.ds(start, cells)],
            own_basis.at[step],
            local_sem.at[step],
        )

    def first_copy(step):
        return remote(
            first_out.at[step],
            first_in.at[step],
            first_send.at[step],
            first_recv.at[step],
            toward(step),
        )

    def along_copy(step):
        return remote(
            along_out.at[step],
            along_in.at[step],
            along_send.at[step],
            along_recv.at[step],
            toward(step),
        )

    def back_copy(step):
        return remote(
            back_out.at[step],
            back_in.at[step],
            back_send.at[step],
            back_recv.at[step],
            away(step),
        )

    def face_copy(which):
        return remote(
            packed.at[which],
            face_in.at[which],
            face_send.at[which],
            face_recv.at[which],
            above if which == 0 else below,
        )

    def links_copy():
        return remote(links, links_in, face_send.at[2], face_recv.at[2], above)

    def stat_copy(step):
        return remote(
            stat_line,
            stat_in.at[step],
            stat_send.at[step],
            stat_recv.at[step],
            {"rows": (row + step) % count},
        )

    def each(first, last, body):
        def run(step, carry):
            body(step)
            return carry

        lax.fori_loop(first, last, run, 0)

    barrier = pltpu.get_barrier_semaphore()

    def greet(where):
        pl.semaphore_signal(barrier, inc=1, device_id=where, device_id_type=pl.DeviceIdType.MESH)

    coefficients_copy = pltpu.make_async_copy(coefficients_in, coefficients, input_sem.at[0])
    coefficients_copy.start()
    each(0, planes, lambda step: local_copy(step).start())
    inputs = [
        pltpu.make_async_copy(source, target, input_sem.at[place + 1])
        for place, (source, target) in enumerate(
            (
                (eigen_in, eigen),
                (used_in, used),
                (lower_in, lower),
                (upper_in, upper),
                (stiffness_in, stiffness),
                (damping_in, damping),
                (mass_in, mass),
            )
        )
    ]
    for copy in inputs:
        copy.start()
    greet({"vecs": (vec + 1) % vecs})
    greet({"vecs": (vec + 3) % vecs})
    each(1, count, lambda step: greet({"rows": (row + step) % count}))

    coefficients_copy.wait()
    total_rank, total_vectors = coefficients.shape[1], coefficients.shape[0]
    rank = iota((total_rank, CHUNKS * DEPTH), 0)
    deep = iota((total_rank, CHUNKS * DEPTH), 1) & (DEPTH - 1)
    pick = ones_where((rank == vec * rank_part + deep) & (deep < rank_part))
    own_rank = jnp.dot(coefficients[...], pick, preferred_element_type=jnp.float32)
    own_rank = own_rank.astype(jnp.bfloat16)
    same_chunk = (iota((held, CHUNKS * DEPTH), 0) & (CHUNKS - 1)) == (
        iota((held, CHUNKS * DEPTH), 1) // DEPTH
    )
    vector = iota((held, total_vectors), 1)
    vector_of = iota((held, total_vectors), 0) // CHUNKS
    for place, ahead in enumerate((2, 1, 0, 3)):
        owner = (vec + ahead) % vecs
        choose = ones_where(vector == owner * vector_part + vector_of)
        part = jnp.dot(choose, own_rank, preferred_element_type=jnp.float32)
        part = jnp.where(same_chunk, part, 0.0).astype(jnp.bfloat16)
        factors[0, place * held : (place + 1) * held] = part
        place = place if place % 2 == 0 else 4 - place
        factors[1, place * held : (place + 1) * held] = part

    unused = jnp.zeros((DEPTH - rank_part, width), jnp.bfloat16)

    def produce(step):
        local_copy(step).wait()
        pieces = []
        for chunk in range(CHUNKS):
            piece = own_basis[step, :, chunk * width : (chunk + 1) * width]
            pieces += [piece, unused]
        stacked = jnp.concatenate(pieces, axis=0)
        role = step % 2

        def part(place):
            return jnp.dot(
                factors[role, place * held : (place + 1) * held],
                stacked,
                preferred_element_type=jnp.float32,
            )

        first_out[step] = part(0).astype(jnp.bfloat16)
        first_copy(step).start()
        middle[step] = part(1)
        values[plane_at(step) + 1] = part(2)
        back_out[step] = part(3).astype(jnp.bfloat16)

    def relay(step):
        first_copy(step).wait_recv()
        for start in range(0, held, PAD):
            rows = slice(start, start + PAD)
            total = middle[step, rows] + first_in[step, rows].astype(jnp.float32)
            along_out[step, rows] = total.astype(jnp.bfloat16)
        along_copy(step).start()
        back_copy(step).start()

    pl.semaphore_wait(barrier, count + 1)
    each(0, LEAD, produce)

    for copy in inputs:
        copy.wait()
    values[0] = jnp.zeros((held, width), jnp.float32)
    values[planes + 1] = jnp.zeros((held, width), jnp.float32)
    stat_out[...] = jnp.zeros_like(stat_out)
    link_sums[...] = jnp.zeros_like(link_sums)

    is_used = iota((1, slots), 1) < used[0]
    links[:, :slots] = jnp.where(is_used, lower[...], -1)
    links[:, slots:] = jnp.where(is_used, upper[...], -1)
    links_copy().start()

    place = iota((CHUNKS * PAD, held), 0)
    source = iota((CHUNKS * PAD, held), 1)
    spread_rows[...] = ones_where(
        ((place // PAD) == (source & (CHUNKS - 1))) & ((place & (PAD - 1)) == (source // CHUNKS))
    )
    chunk_ones[...] = ones_where(
        (iota((held, held), 0) // CHUNKS) == (iota((held, held), 1) // CHUNKS)
    )
    diag = (iota((held, vector_part), 0) // CHUNKS) == iota((held, vector_part), 1)
    lam = jnp.where(diag, jnp.broadcast_to(eigen[...], (held, vector_part)), 0.0)
    lam = jnp.broadcast_to(jnp.sum(lam, axis=1, keepdims=True), (held, LANES))
    lam_of[0] = lam
    lam_of[1] = lam * lam
    lam_of[2] = lam * lam * 0.1 + lam * 0.3 + 1.0

    def fold(block):
        total = block[:, :LANES]
        for start in range(LANES, block.shape[1], LANES):
            total = total + block[:, start : start + LANES]
        return total

    def write(out, plane, block):
        moved = jnp.dot(spread_rows[...], block, preferred_element_type=jnp.float32)
        for chunk in range(CHUNKS):
            start = pl.multiple_of(plane * cells + chunk * width, width)
            piece = moved[chunk * PAD : (chunk + 1) * PAD].astype(jnp.bfloat16)
            out[:, pl.ds(start, width)] = piece[:vector_part]

    def finish(step):
        plane = plane_at(step)
        along_copy(step).wait_recv()
        back_copy(step).wait_recv()
        for start in range(0, held, PAD):
            rows = slice(start, start + PAD)
            total = values[plane + 1, rows] + along_in[step, rows].astype(jnp.float32)
            total = total + back_in[step, rows].astype(jnp.float32)
            rounded = total.astype(jnp.bfloat16)
            exact = rounded.astype(jnp.float32)
            values[plane + 1, rows] = exact
            packed[step, rows] = rounded
            stat_out[rows] += fold(exact * exact)
        write(eig_out, plane, packed[step])

    column = iota((PAD, LANES), 1)
    not_left = (column & (WID - 1)) != 0
    not_right = (column & (WID - 1)) != WID - 1
    low_half = column < WID
    chunk_of = iota((PAD, LANES), 0) & (CHUNKS - 1)
    not_first = chunk_of != 0
    not_last = chunk_of != CHUNKS - 1

    def stencil(plane, link):
        diagonals = []
        for part in range(parts):
            at = pl.ds(plane * plane_rows + part, CHUNKS, stride=parts)
            diagonals.append(
                [jnp.concatenate([array[at]] * 2, axis=0) for array in (mass, damping, stiffness)]
            )
        for start in range(0, held, PAD):
            rows = slice(start, start + PAD)
            lam = lam_of[0, rows]
            lam_sq = lam_of[1, rows]
            coupling = lam_of[2, rows]
            mids = [
                values[plane + 1, rows, part * LANES : (part + 1) * LANES] for part in range(parts)
            ]
            swapped = [pltpu.roll(mid, WID, 1) for mid in mids]
            before = jnp.where(not_first, pltpu.roll(swapped[-1], 1, 0), 0.0)
            after = jnp.where(not_last, pltpu.roll(swapped[0], PAD - 1, 0), 0.0)
            swapped = [before, *swapped, after]
            squares = jnp.zeros((PAD, LANES), jnp.float32)
            for part in range(parts):
                lanes = slice(part * LANES, (part + 1) * LANES)
                mid = mids[part]
                total = values[plane, rows, lanes] + values[plane + 2, rows, lanes]
                total = total + (
                    swapped[part + 1] + jnp.where(low_half, swapped[part], swapped[part + 2])
                )
                total = total + jnp.where(not_right, pltpu.roll(mid, LANES - 1, 1), 0.0)
                total = total + jnp.where(not_left, pltpu.roll(mid, 1, 1), 0.0)
                if link is not None:
                    at = part * held + start
                    total = total + link_sums[link, at : at + PAD]
                mass_b, damping_b, stiffness_b = diagonals[part]
                diagonal = lam_sq * mass_b + lam * damping_b + stiffness_b
                full = diagonal * mid - coupling * total
                res_packed[rows, lanes] = full.astype(jnp.bfloat16)
                squares = squares + full * full
            at = slice(held + start, held + start + PAD)
            stat_out[at] += squares
        write(res_out, plane, res_packed[...])

    low_iota = iota((LANES, BLOCK), 0)
    row_chunk = iota((held, BLOCK), 0) & (CHUNKS - 1)

    def link_side(which, lists, source_row, target_row, step):
        stacked = jnp.concatenate(
            [face_in[which, :, part * LANES : (part + 1) * LANES] for part in range(parts)], axis=0
        )
        source = lists[:, pl.ds(pl.multiple_of(source_row * slots + step * BLOCK, BLOCK), BLOCK)]
        target = lists[:, pl.ds(pl.multiple_of(target_row * slots + step * BLOCK, BLOCK), BLOCK)]
        low = ones_where(low_iota == (source & (LANES - 1)))
        picked = jnp.dot(stacked, low, preferred_element_type=jnp.float32)
        high = jnp.broadcast_to(source >> 7, (held, BLOCK))
        got = jnp.zeros((held, BLOCK), jnp.float32)
        for part in range(parts):
            mine = high == row_chunk * parts + part
            got = got + jnp.where(mine, picked[part * held : (part + 1) * held], 0.0)
        got = jnp.dot(
            chunk_ones[...], got.astype(jnp.bfloat16), preferred_element_type=jnp.float32
        )
        high = jnp.broadcast_to(target >> 7, (held, BLOCK))
        placed = jnp.concatenate(
            [
                jnp.where(high == row_chunk * parts + part, got, 0.0).astype(jnp.bfloat16)
                for part in range(parts)
            ],
            axis=0,
        )
        low = ones_where(low_iota == (target & (LANES - 1)))
        link_sums[which] += lax.dot_general(
            placed, low, (((1,), (1,)), ((), ())), preferred_element_type=jnp.float32
        )

    def advance(step):
        @pl.when(step + LEAD < planes)
        def _():
            produce(step + LEAD)

        @pl.when(step < planes)
        def _():
            relay(step)

        @pl.when(step >= LAG)
        def _():
            finish(step - LAG)

            @pl.when(step == LAG)
            def _():
                face_copy(0).start()

            @pl.when(step == LAG + 1)
            def _():
                face_copy(1).start()

        @pl.when(step >= LAG + 3)
        def _():
            stencil(step - LAG - 2, None)

        @pl.when(step == LINKS_AT)
        def _():
            face_copy(0).wait_recv()
            face_copy(1).wait_recv()
            links_copy().wait_recv()

        @pl.when((step >= LINKS_AT) & (step < LINKS_AT + slots // BLOCK))
        def _():
            link_side(0, links_in, 0, 1, step - LINKS_AT)
            link_side(1, links, 1, 0, step - LINKS_AT)

        @pl.when(step == LINKS_AT + slots // BLOCK)
        def _():
            stencil(0, 0)

    each(0, planes + LAG, advance)
    stencil(planes - 2, None)
    stencil(planes - 1, 1)

    sums = jnp.sum(stat_out[...].reshape(2 * vector_part, CHUNKS, LANES), axis=1)
    sums = jnp.sum(sums, axis=1, keepdims=True)
    spot = iota((2 * vector_part, LANES), 0) == iota((2 * vector_part, LANES), 1)
    line = jnp.sum(jnp.where(spot, sums, 0.0), axis=0, keepdims=True)
    stat_line[...] = line
    each(1, count, lambda step: stat_copy(step).start())

    def sent(step):
        first_copy(step).wait_send()
        along_copy(step).wait_send()
        back_copy(step).wait_send()

    each(0, planes, sent)
    links_copy().wait_send()
    face_copy(0).wait_send()
    face_copy(1).wait_send()
    each(1, count, lambda step: stat_copy(step).wait_recv())
    for step in range(1, count):
        line = line + stat_in[step]
    norms = jnp.sqrt(line[:, vector_part : 2 * vector_part]) / jnp.sqrt(line[:, :vector_part] + 1.0)
    norm_out[...] = norms
    each(1, count, lambda step: stat_copy(step).wait_send())


def write_back(eig_held, res_held, norm_held, eig_out, res_out, norm_out, sem):
    copies = [
        pltpu.make_async_copy(source, target, sem.at[place])
        for place, (source, target) in enumerate(
            ((eig_held, eig_out), (res_held, res_out), (norm_held, norm_out))
        )
    ]
    for copy in copies:
        copy.start()
    for copy in copies:
        copy.wait()


def on_device(
    basis,
    coefficients,
    eigen_values,
    stiffness,
    damping,
    mass,
    link_count,
    lower_cells,
    upper_cells,
):
    count = lax.axis_size("rows")
    vector_part = eigen_values.shape[0]
    rank_part, rows_local = basis.shape
    cells = WID * WID
    planes = rows_local // cells
    slots = lower_cells.shape[1]
    held = vector_part * CHUNKS
    width = cells // CHUNKS
    vmem = pl.BlockSpec(memory_space=pltpu.VMEM)
    anywhere = pl.BlockSpec(memory_space=pltpu.HBM)
    dma = pltpu.SemaphoreType.DMA
    wire = pltpu.VMEM((planes, held, width), jnp.bfloat16)
    eigvecs, residuals, norms = pl.pallas_call(
        functools.partial(kernel, count, planes, cells, vector_part, rank_part),
        out_shape=(
            pltpu.VMEM((vector_part, rows_local), jnp.bfloat16),
            pltpu.VMEM((vector_part, rows_local), jnp.bfloat16),
            pltpu.VMEM((1, vector_part), jnp.float32),
        ),
        in_specs=[anywhere] * 9,
        out_specs=(vmem, vmem, vmem),
        scratch_shapes=[
            pltpu.VMEM((planes, rank_part, cells), jnp.bfloat16),
            wire,
            wire,
            wire,
            wire,
            wire,
            wire,
            pltpu.VMEM((planes, held, width), jnp.float32),
            pltpu.VMEM((planes + 2, held, width), jnp.float32),
            wire,
            pltpu.VMEM((held, width), jnp.bfloat16),
            pltpu.VMEM((2, held, width), jnp.bfloat16),
            pltpu.VMEM((1, 2 * slots), jnp.int32),
            pltpu.VMEM((1, 2 * slots), jnp.int32),
            pltpu.VMEM((2, width // LANES * held, LANES), jnp.float32),
            pltpu.VMEM((2 * held, LANES), jnp.float32),
            pltpu.VMEM((count, 1, LANES), jnp.float32),
            pltpu.VMEM((1, LANES), jnp.float32),
            pltpu.VMEM((2, 4 * held, CHUNKS * DEPTH), jnp.bfloat16),
            pltpu.VMEM((CHUNKS * PAD, held), jnp.bfloat16),
            pltpu.VMEM((held, held), jnp.bfloat16),
            pltpu.VMEM((3, held, LANES), jnp.float32),
            pltpu.VMEM((rows_local // LANES, LANES), jnp.float32),
            pltpu.VMEM((rows_local // LANES, LANES), jnp.float32),
            pltpu.VMEM((rows_local // LANES, LANES), jnp.float32),
            pltpu.VMEM(coefficients.shape[::-1], jnp.bfloat16),
            pltpu.VMEM((1, vector_part), jnp.float32),
            pltpu.SMEM((1,), jnp.int32),
            pltpu.VMEM((1, slots), jnp.int32),
            pltpu.VMEM((1, slots), jnp.int32),
            dma((8,)),
            dma((planes,)),
            dma((planes,)),
            dma((planes,)),
            dma((planes,)),
            dma((planes,)),
            dma((planes,)),
            dma((planes,)),
            dma((3,)),
            dma((3,)),
            dma((count,)),
            dma((count,)),
        ],
        compiler_params=pltpu.CompilerParams(
            collective_id=0, has_side_effects=True, vmem_limit_bytes=56 * 1024 * 1024
        ),
    )(
        basis,
        coefficients.T,
        eigen_values[None, :],
        stiffness.reshape(-1, LANES),
        damping.reshape(-1, LANES),
        mass.reshape(-1, LANES),
        link_count,
        lower_cells,
        upper_cells,
    )
    eigvecs, residuals, norms = pl.pallas_call(
        write_back,
        out_shape=tuple(
            jax.ShapeDtypeStruct(held.shape, held.dtype) for held in (eigvecs, residuals, norms)
        ),
        in_specs=[vmem] * 3,
        out_specs=[pl.BlockSpec(memory_space=pl.ANY)] * 3,
        scratch_shapes=[dma((3,))],
        compiler_params=pltpu.CompilerParams(vmem_limit_bytes=1 << 20),
    )(eigvecs, residuals, norms)
    return eigvecs, residuals, norms[0]


def solution(mesh):
    placed = (
        P("vecs", "rows"),
        P(),
        P("vecs"),
        P("rows"),
        P("rows"),
        P("rows"),
        P("rows"),
        P("rows", None),
        P("rows", None),
    )
    return jax.shard_map(
        on_device,
        mesh=mesh,
        in_specs=placed,
        out_specs=(P("vecs", "rows"), P("vecs", "rows"), P("vecs")),
        check_vma=False,
    )
```

time: 140 us -> 66.9 us (0.48)
  Pallas kernels: 139 us -> 65.5 us
    pallas_call x1, Pallas kernels: 137 us -> 63.4 us  [on_device(): pl.pallas_call(functools.partial(kernel, count, planes, cells, vector_par...]
where the time goes in v1:
time: 66.9 us; the launch traced here: 66.8 us
  Pallas kernels  65.5 us (98%)
  between operations  1.29 us (2%)
    pallas_call x1, Pallas kernels, on_device(): pl.pallas_call(functools.partial(kernel, count, planes, cells, vector_par...  63.4 us
    pallas_call x1, Pallas kernels, on_device(): pl.pallas_call(write_back, out_shape=tuple((jax.ShapeDtypeStruct(held.sha...  2.04 us

profile of v1, /device:TPU:1, one launch (start us, length us, event | category | flops | bytes accessed | tf_op | source)
XLA Modules:
  0.0 66.8 jit_solution(5993856889577016014)
XLA Ops:
  1.3 63.4 %shard_map.112 = (bf16[10,65536]{1,0:T(8,128)(2,1)S(1)}, bf16[10,65536]{1,0:T(8,128)(2,1)S(1)}, f32[1,10]{1,0:T(1,128)S(1)}) custom-call(bf16[25,65536]{1,0:T(8,128)(2,1)} %basis.1, bf16[40,100]{1,0:T(8,128)(2,1)} %bitcast.9, f32[1,10]{1,0:T(1,128)} %bitcast.10, f32[512,128]{1,0:T(8,128)} %bitcast.6, f32[512,128]{1,0:T(8,128)} %bitcast.7, ...), custom_call_target="tpu_custom_call" | custom-call | tf_op jit(solution)/shard_map/pallas_call | solution.py:509
  64.7 2.0 %shard_map.113 = (bf16[10,65536]{1,0:T(8,128)(2,1)}, bf16[10,65536]{1,0:T(8,128)(2,1)}, f32[1,10]{1,0:T(1,128)}) custom-call(bf16[10,65536]{1,0:T(8,128)(2,1)S(1)} %get-tuple-element.9.eig_held, bf16[10,65536]{1,0:T(8,128)(2,1)S(1)} %get-tuple-element.10.res_held, f32[1,10]{1,0:T(1,128)S(1)} %get-tuple-element.11.norm_held), custom_call_target="tpu_custom_call" | custom-call | tf_op jit(solution)/shard_map/pallas_call | solution.py:576

commit v2 on v1

--- a/solution.py
+++ b/solution.py
@@ -15,7 +15,7 @@
 BLOCK = 512
 LEAD = 6
 LAG = 2
-LINKS_AT = 7
+LINKS_AT = 6
 
 
 def remote(src, dst, send_sem, recv_sem, where):
@@ -97,6 +97,7 @@
     face_recv,
     stat_send,
     stat_recv,
+    meet_sem,
 ):
     row = lax.axis_index("rows")
     vec = lax.axis_index("vecs")
@@ -207,7 +208,17 @@
         copy.start()
     greet({"vecs": (vec + 1) % vecs})
     greet({"vecs": (vec + 3) % vecs})
-    each(1, count, lambda step: greet({"rows": (row + step) % count}))
+    greet(above)
+    greet(below)
+
+    def meet(round_):
+        for where in (row + 2**round_, row + count - 2**round_):
+            pl.semaphore_signal(
+                meet_sem.at[round_],
+                inc=1,
+                device_id={"rows": where % count},
+                device_id_type=pl.DeviceIdType.MESH,
+            )
 
     coefficients_copy.wait()
     total_rank, total_vectors = coefficients.shape[1], coefficients.shape[0]
@@ -263,7 +274,8 @@
         along_copy(step).start()
         back_copy(step).start()
 
-    pl.semaphore_wait(barrier, count + 1)
+    pl.semaphore_wait(barrier, 4)
+    meet(0)
     each(0, LEAD, produce)
 
     for copy in inputs:
@@ -273,7 +285,7 @@
     stat_out[...] = jnp.zeros_like(stat_out)
     link_sums[...] = jnp.zeros_like(link_sums)
 
-    is_used = iota((1, slots), 1) < used[0]
+    is_used = iota((1, slots), 1) < used[...]
     links[:, :slots] = jnp.where(is_used, lower[...], -1)
     links[:, slots:] = jnp.where(is_used, upper[...], -1)
     links_copy().start()
@@ -319,7 +331,12 @@
             values[plane + 1, rows] = exact
             packed[step, rows] = rounded
             stat_out[rows] += fold(exact * exact)
-        write(eig_out, plane, packed[step])
+
+    def write_eig(step):
+        write(eig_out, plane_at(step), packed[step])
+
+    def write_res(plane, slot):
+        write(res_out, plane, res_packed[slot])
 
     column = iota((PAD, LANES), 1)
     not_left = (column & (WID - 1)) != 0
@@ -329,7 +346,7 @@
     not_first = chunk_of != 0
     not_last = chunk_of != CHUNKS - 1
 
-    def stencil(plane, link):
+    def stencil(plane, link, slot=0):
         diagonals = []
         for part in range(parts):
             at = pl.ds(plane * plane_rows + part, CHUNKS, stride=parts)
@@ -364,45 +381,65 @@
                 mass_b, damping_b, stiffness_b = diagonals[part]
                 diagonal = lam_sq * mass_b + lam * damping_b + stiffness_b
                 full = diagonal * mid - coupling * total
-                res_packed[rows, lanes] = full.astype(jnp.bfloat16)
+                res_packed[slot, rows, lanes] = full.astype(jnp.bfloat16)
                 squares = squares + full * full
             at = slice(held + start, held + start + PAD)
             stat_out[at] += squares
-        write(res_out, plane, res_packed[...])
 
     low_iota = iota((LANES, BLOCK), 0)
     row_chunk = iota((held, BLOCK), 0) & (CHUNKS - 1)
 
-    def link_side(which, lists, source_row, target_row, step):
-        stacked = jnp.concatenate(
-            [face_in[which, :, part * LANES : (part + 1) * LANES] for part in range(parts)], axis=0
-        )
-        source = lists[:, pl.ds(pl.multiple_of(source_row * slots + step * BLOCK, BLOCK), BLOCK)]
-        target = lists[:, pl.ds(pl.multiple_of(target_row * slots + step * BLOCK, BLOCK), BLOCK)]
-        low = ones_where(low_iota == (source & (LANES - 1)))
-        picked = jnp.dot(stacked, low, preferred_element_type=jnp.float32)
-        high = jnp.broadcast_to(source >> 7, (held, BLOCK))
-        got = jnp.zeros((held, BLOCK), jnp.float32)
-        for part in range(parts):
-            mine = high == row_chunk * parts + part
-            got = got + jnp.where(mine, picked[part * held : (part + 1) * held], 0.0)
-        got = jnp.dot(
-            chunk_ones[...], got.astype(jnp.bfloat16), preferred_element_type=jnp.float32
-        )
-        high = jnp.broadcast_to(target >> 7, (held, BLOCK))
-        placed = jnp.concatenate(
-            [
-                jnp.where(high == row_chunk * parts + part, got, 0.0).astype(jnp.bfloat16)
-                for part in range(parts)
-            ],
-            axis=0,
-        )
-        low = ones_where(low_iota == (target & (LANES - 1)))
-        link_sums[which] += lax.dot_general(
-            placed, low, (((1,), (1,)), ((), ())), preferred_element_type=jnp.float32
-        )
+    sides = ((0, links_in, 0, 1), (1, links, 1, 0))
+
+    def link_block(step):
+        start = pl.multiple_of(step * BLOCK, BLOCK)
+        targets, picked, got = [], [], []
+        for which, lists, source_row, target_row in sides:
+            stacked = jnp.concatenate(
+                [face_in[which, :, part * LANES : (part + 1) * LANES] for part in range(parts)],
+                axis=0,
+            )
+            source = lists[:, pl.ds(source_row * slots + start, BLOCK)]
+            targets.append(lists[:, pl.ds(target_row * slots + start, BLOCK)])
+            low = ones_where(low_iota == (source & (LANES - 1)))
+            rows = jnp.dot(stacked, low, preferred_element_type=jnp.float32)
+            picked.append((source, rows))
+        for source, rows in picked:
+            high = jnp.broadcast_to(source >> 7, (held, BLOCK))
+            total = jnp.zeros((held, BLOCK), jnp.float32)
+            for part in range(parts):
+                mine = high == row_chunk * parts + part
+                total = total + jnp.where(mine, rows[part * held : (part + 1) * held], 0.0)
+            got.append(
+                jnp.dot(
+                    chunk_ones[...], total.astype(jnp.bfloat16), preferred_element_type=jnp.float32
+                )
+            )
+        for (which, *_), target, value in zip(sides, targets, got):
+            high = jnp.broadcast_to(target >> 7, (held, BLOCK))
+            placed = jnp.concatenate(
+                [
+                    jnp.where(high == row_chunk * parts + part, value, 0.0).astype(jnp.bfloat16)
+                    for part in range(parts)
+                ],
+                axis=0,
+            )
+            low = ones_where(low_iota == (target & (LANES - 1)))
+            link_sums[which] += lax.dot_general(
+                placed, low, (((1,), (1,)), ((), ())), preferred_element_type=jnp.float32
+            )
+
+    rounds = meet_sem.shape[0]
 
     def advance(step):
+        for round_ in range(rounds):
+
+            @pl.when(step == 2 * round_ + 1)
+            def _():
+                pl.semaphore_wait(meet_sem.at[round_], 2)
+                if round_ + 1 < rounds:
+                    meet(round_ + 1)
+
         @pl.when(step + LEAD < planes)
         def _():
             produce(step + LEAD)
@@ -415,6 +452,8 @@
         def _():
             finish(step - LAG)
 
+            write_eig(step - LAG)
+
             @pl.when(step == LAG)
             def _():
                 face_copy(0).start()
@@ -426,6 +465,7 @@
         @pl.when(step >= LAG + 3)
         def _():
             stencil(step - LAG - 2, None)
+            write_res(step - LAG - 2, 0)
 
         @pl.when(step == LINKS_AT)
         def _():
@@ -435,23 +475,28 @@
 
         @pl.when((step >= LINKS_AT) & (step < LINKS_AT + slots // BLOCK))
         def _():
-            link_side(0, links_in, 0, 1, step - LINKS_AT)
-            link_side(1, links, 1, 0, step - LINKS_AT)
+            link_block(step - LINKS_AT)
 
         @pl.when(step == LINKS_AT + slots // BLOCK)
         def _():
             stencil(0, 0)
-
-    each(0, planes + LAG, advance)
-    stencil(planes - 2, None)
-    stencil(planes - 1, 1)
+            write_res(0, 0)
+
+    last = planes - 1
+    each(0, last + LAG, advance)
+    finish(last)
+    for slot in range(3):
+        stencil(last - 2 + slot, 1 if slot == 2 else None, slot)
 
     sums = jnp.sum(stat_out[...].reshape(2 * vector_part, CHUNKS, LANES), axis=1)
     sums = jnp.sum(sums, axis=1, keepdims=True)
     spot = iota((2 * vector_part, LANES), 0) == iota((2 * vector_part, LANES), 1)
     line = jnp.sum(jnp.where(spot, sums, 0.0), axis=0, keepdims=True)
     stat_line[...] = line
-    each(1, count, lambda step: stat_copy(step).start())
+    each(0, count - 1, lambda step: stat_copy(1 + (step + 11) % (count - 1)).start())
+    write_eig(last)
+    for slot in range(3):
+        write_res(last - 2 + slot, slot)
 
     def sent(step):
         first_copy(step).wait_send()
@@ -502,6 +547,7 @@
     slots = lower_cells.shape[1]
     held = vector_part * CHUNKS
     width = cells // CHUNKS
+    rounds = (count // 2 - 1).bit_length()
     vmem = pl.BlockSpec(memory_space=pltpu.VMEM)
     anywhere = pl.BlockSpec(memory_space=pltpu.HBM)
     dma = pltpu.SemaphoreType.DMA
@@ -526,7 +572,7 @@
             pltpu.VMEM((planes, held, width), jnp.float32),
             pltpu.VMEM((planes + 2, held, width), jnp.float32),
             wire,
-            pltpu.VMEM((held, width), jnp.bfloat16),
+            pltpu.VMEM((3, held, width), jnp.bfloat16),
             pltpu.VMEM((2, held, width), jnp.bfloat16),
             pltpu.VMEM((1, 2 * slots), jnp.int32),
             pltpu.VMEM((1, 2 * slots), jnp.int32),
@@ -543,7 +589,7 @@
             pltpu.VMEM((rows_local // LANES, LANES), jnp.float32),
             pltpu.VMEM(coefficients.shape[::-1], jnp.bfloat16),
             pltpu.VMEM((1, vector_part), jnp.float32),
-            pltpu.SMEM((1,), jnp.int32),
+            pltpu.VMEM((1, 1), jnp.int32),
             pltpu.VMEM((1, slots), jnp.int32),
             pltpu.VMEM((1, slots), jnp.int32),
             dma((8,)),
@@ -558,6 +604,7 @@
             dma((3,)),
             dma((count,)),
             dma((count,)),
+            pltpu.SemaphoreType.REGULAR((rounds,)),
         ],
         compiler_params=pltpu.CompilerParams(
             collective_id=0, has_side_effects=True, vmem_limit_bytes=56 * 1024 * 1024
@@ -569,7 +616,7 @@
         stiffness.reshape(-1, LANES),
         damping.reshape(-1, LANES),
         mass.reshape(-1, LANES),
-        link_count,
+        link_count[None, :],
         lower_cells,
         upper_cells,
     )

time: 66.9 us -> 64.5 us (0.964)
  Pallas kernels: 65.5 us -> 63.1 us
    pallas_call x1, Pallas kernels: 63.4 us -> 61.1 us  [on_device(): pl.pallas_call(functools.partial(kernel, count, planes, cells, vector_par...]
where the time goes in v2:
time: 64.5 us; the launch traced here: 64.4 us
  Pallas kernels  63.1 us (98%)
  between operations  1.29 us (2%)
    pallas_call x1, Pallas kernels, on_device(): pl.pallas_call(functools.partial(kernel, count, planes, cells, vector_par...  61.1 us
    pallas_call x1, Pallas kernels, on_device(): pl.pallas_call(write_back, out_shape=tuple((jax.ShapeDtypeStruct(held.sha...  2.04 us

profile of v2, /device:TPU:1, one launch (start us, length us, event | category | flops | bytes accessed | tf_op | source)
XLA Modules:
  0.0 64.4 jit_solution(11326363128794711801)
XLA Ops:
  1.3 61.1 %shard_map.112 = (bf16[10,65536]{1,0:T(8,128)(2,1)S(1)}, bf16[10,65536]{1,0:T(8,128)(2,1)S(1)}, f32[1,10]{1,0:T(1,128)S(1)}) custom-call(bf16[25,65536]{1,0:T(8,128)(2,1)} %basis.1, bf16[40,100]{1,0:T(8,128)(2,1)} %bitcast.11, f32[1,10]{1,0:T(1,128)} %bitcast.12, f32[512,128]{1,0:T(8,128)} %bitcast.8, f32[512,128]{1,0:T(8,128)} %bitcast.9, ...), custom_call_target="tpu_custom_call" | custom-call | tf_op jit(solution)/shard_map/pallas_call | solution.py:555
  62.3 2.0 %shard_map.113 = (bf16[10,65536]{1,0:T(8,128)(2,1)}, bf16[10,65536]{1,0:T(8,128)(2,1)}, f32[1,10]{1,0:T(1,128)}) custom-call(bf16[10,65536]{1,0:T(8,128)(2,1)S(1)} %get-tuple-element.9.eig_held, bf16[10,65536]{1,0:T(8,128)(2,1)S(1)} %get-tuple-element.10.res_held, f32[1,10]{1,0:T(1,128)S(1)} %get-tuple-element.11.norm_held), custom_call_target="tpu_custom_call" | custom-call | tf_op jit(solution)/shard_map/pallas_call | solution.py:623

commit v3 on v2

--- a/solution.py
+++ b/solution.py
@@ -13,9 +13,7 @@
 DEPTH = 32
 PAD = 16
 BLOCK = 512
-LEAD = 6
-LAG = 2
-LINKS_AT = 6
+VECS = 4
 
 
 def remote(src, dst, send_sem, recv_sem, where):
@@ -56,24 +54,27 @@
     res_out,
     norm_out,
     own_basis,
-    first_out,
-    first_in,
-    along_out,
-    along_in,
-    back_out,
-    back_in,
-    middle,
+    tail_out,
+    raw_in,
+    tail_in,
+    mid_out,
+    mid_in,
+    keep,
+    last_out,
+    last_in,
     values,
     packed,
     res_packed,
     face_in,
     links_in,
     links,
+    hot,
     link_sums,
     stat_out,
     stat_in,
     stat_line,
-    factors,
+    own_factors,
+    mate_factors,
     spread_rows,
     chunk_ones,
     lam_of,
@@ -87,12 +88,12 @@
     upper,
     input_sem,
     local_sem,
-    first_send,
-    first_recv,
-    along_send,
-    along_recv,
-    back_send,
-    back_recv,
+    raw_send,
+    raw_recv,
+    mid_send,
+    mid_recv,
+    last_send,
+    last_recv,
     face_send,
     face_recv,
     stat_send,
@@ -101,7 +102,6 @@
 ):
     row = lax.axis_index("rows")
     vec = lax.axis_index("vecs")
-    vecs = 4
     above = {"rows": (row + 1) % count}
     below = {"rows": (row + count - 1) % count}
     slots = links.shape[1] // 2
@@ -109,15 +109,23 @@
     parts = width // LANES
     held = vector_part * CHUNKS
     plane_rows = cells // LANES
+    whole = rank_part // CHUNKS * CHUNKS
+    turns = planes // VECS
 
     def plane_at(step):
         return (step + planes - 1) % planes
 
-    def toward(step):
-        return {"vecs": (vec + 1 + 2 * (step % 2)) % vecs}
-
-    def away(step):
-        return {"vecs": (vec + 3 - 2 * (step % 2)) % vecs}
+    def outer_at(turn, side):
+        return turn * VECS + (vec + side) % VECS
+
+    def inner_at(turn, side):
+        return turn * VECS + (vec + 3 - side) % VECS
+
+    def inward(side):
+        return {"vecs": (vec + 1 + 2 * side) % VECS}
+
+    def outward(side):
+        return {"vecs": (vec + 3 - 2 * side) % VECS}
 
     def local_copy(step):
         start = pl.multiple_of(plane_at(step) * cells, cells)
@@ -127,31 +135,46 @@
             local_sem.at[step],
         )
 
-    def first_copy(step):
+    def raw_copy(turn, side, half):
+        place = turn * 2 + side
+        lanes = pl.ds(half * (cells // 2), cells // 2)
         return remote(
-            first_out.at[step],
-            first_in.at[step],
-            first_send.at[step],
-            first_recv.at[step],
-            toward(step),
-        )
-
-    def along_copy(step):
+            own_basis.at[outer_at(turn, side), pl.ds(0, whole), lanes],
+            raw_in.at[place, :, lanes],
+            raw_send.at[half, place],
+            raw_recv.at[half, place],
+            inward(side),
+        )
+
+    def tail_copy(turn, side):
+        place = turn * 2 + side
         return remote(
-            along_out.at[step],
-            along_in.at[step],
-            along_send.at[step],
-            along_recv.at[step],
-            toward(step),
-        )
-
-    def back_copy(step):
+            tail_out.at[place],
+            tail_in.at[place],
+            raw_send.at[2, place],
+            raw_recv.at[2, place],
+            inward(side),
+        )
+
+    def mid_copy(turn, side):
+        place = turn * 2 + side
+        other = turn * 2 + 1 - side
         return remote(
-            back_out.at[step],
-            back_in.at[step],
-            back_send.at[step],
-            back_recv.at[step],
-            away(step),
+            mid_out.at[place],
+            mid_in.at[other],
+            mid_send.at[place],
+            mid_recv.at[other],
+            inward(side),
+        )
+
+    def last_copy(turn, side):
+        place = turn * 2 + side
+        return remote(
+            last_out.at[place],
+            last_in.at[place],
+            last_send.at[place],
+            last_recv.at[place],
+            outward(side),
         )
 
     def face_copy(which):
@@ -189,7 +212,14 @@
 
     coefficients_copy = pltpu.make_async_copy(coefficients_in, coefficients, input_sem.at[0])
     coefficients_copy.start()
-    each(0, planes, lambda step: local_copy(step).start())
+
+    def load(turn):
+        for side in range(2):
+            local_copy(outer_at(turn, side)).start()
+        for side in range(2):
+            local_copy(inner_at(turn, side)).start()
+
+    each(0, turns, load)
     inputs = [
         pltpu.make_async_copy(source, target, input_sem.at[place + 1])
         for place, (source, target) in enumerate(
@@ -206,8 +236,8 @@
     ]
     for copy in inputs:
         copy.start()
-    greet({"vecs": (vec + 1) % vecs})
-    greet({"vecs": (vec + 3) % vecs})
+    greet({"vecs": (vec + 1) % VECS})
+    greet({"vecs": (vec + 3) % VECS})
     greet(above)
     greet(below)
 
@@ -220,63 +250,111 @@
                 device_id_type=pl.DeviceIdType.MESH,
             )
 
+    unused = jnp.zeros((DEPTH - rank_part, width), jnp.bfloat16)
+    deep = CHUNKS * DEPTH
+    column = iota((CHUNKS, deep), 1)
+    pick_tail = ones_where(column == iota((CHUNKS, deep), 0) * DEPTH + whole)
+
+    def stack_own(step):
+        pieces = []
+        for chunk in range(CHUNKS):
+            pieces += [own_basis[step, :, chunk * width : (chunk + 1) * width], unused]
+        return jnp.concatenate(pieces, axis=0)
+
+    def send_half(turn, half):
+        def send(side):
+            if half == 0:
+                local_copy(outer_at(turn, side)).wait()
+            raw_copy(turn, side, half).start()
+
+        each(0, 2, send)
+
+    def send_tail(turn):
+        def send(side):
+            tail = jnp.dot(
+                pick_tail, stack_own(outer_at(turn, side)), preferred_element_type=jnp.float32
+            )
+            tail_out[turn * 2 + side] = tail.astype(jnp.bfloat16)
+            tail_copy(turn, side).start()
+
+        each(0, 2, send)
+
+    pl.semaphore_wait(barrier, 4)
+    meet(0)
+    for turn in range(2):
+        send_half(turn, 0)
+        send_half(turn, 1)
+        send_tail(turn)
+
     coefficients_copy.wait()
     total_rank, total_vectors = coefficients.shape[1], coefficients.shape[0]
-    rank = iota((total_rank, CHUNKS * DEPTH), 0)
-    deep = iota((total_rank, CHUNKS * DEPTH), 1) & (DEPTH - 1)
-    pick = ones_where((rank == vec * rank_part + deep) & (deep < rank_part))
-    own_rank = jnp.dot(coefficients[...], pick, preferred_element_type=jnp.float32)
-    own_rank = own_rank.astype(jnp.bfloat16)
-    same_chunk = (iota((held, CHUNKS * DEPTH), 0) & (CHUNKS - 1)) == (
-        iota((held, CHUNKS * DEPTH), 1) // DEPTH
-    )
+    rank = iota((total_rank, deep), 0)
+    column = iota((total_rank, deep), 1)
+    own_chunk = column // DEPTH
+    own_depth = column & (DEPTH - 1)
+    mate_chunk = jnp.zeros_like(column)
+    for chunk in range(1, CHUNKS):
+        mate_chunk = mate_chunk + (column >= chunk * whole).astype(jnp.int32)
+    in_tail = column >= CHUNKS * whole
+    mate_depth = jnp.where(in_tail, whole, column - mate_chunk * whole)
+    mate_chunk = jnp.where(in_tail, column - CHUNKS * whole, mate_chunk)
+
+    def factor_rows(chunk, depth, source):
+        pick = ones_where((rank == source * rank_part + depth) & (depth < rank_part))
+        ranks = jnp.dot(coefficients[...], pick, preferred_element_type=jnp.float32)
+        ranks = ranks.astype(jnp.bfloat16)
+        same_chunk = (iota((held, deep), 0) & (CHUNKS - 1)) == chunk[:held]
+
+        def of_owner(owner):
+            choose = ones_where(vector == owner * vector_part + vector_of)
+            part = jnp.dot(choose, ranks, preferred_element_type=jnp.float32)
+            return jnp.where(same_chunk, part, 0.0).astype(jnp.bfloat16)
+
+        return of_owner
+
     vector = iota((held, total_vectors), 1)
     vector_of = iota((held, total_vectors), 0) // CHUNKS
-    for place, ahead in enumerate((2, 1, 0, 3)):
-        owner = (vec + ahead) % vecs
-        choose = ones_where(vector == owner * vector_part + vector_of)
-        part = jnp.dot(choose, own_rank, preferred_element_type=jnp.float32)
-        part = jnp.where(same_chunk, part, 0.0).astype(jnp.bfloat16)
-        factors[0, place * held : (place + 1) * held] = part
-        place = place if place % 2 == 0 else 4 - place
-        factors[1, place * held : (place + 1) * held] = part
-
-    unused = jnp.zeros((DEPTH - rank_part, width), jnp.bfloat16)
-
-    def produce(step):
-        local_copy(step).wait()
-        pieces = []
-        for chunk in range(CHUNKS):
-            piece = own_basis[step, :, chunk * width : (chunk + 1) * width]
-            pieces += [piece, unused]
-        stacked = jnp.concatenate(pieces, axis=0)
-        role = step % 2
-
-        def part(place):
-            return jnp.dot(
-                factors[role, place * held : (place + 1) * held],
-                stacked,
-                preferred_element_type=jnp.float32,
-            )
-
-        first_out[step] = part(0).astype(jnp.bfloat16)
-        first_copy(step).start()
-        middle[step] = part(1)
-        values[plane_at(step) + 1] = part(2)
-        back_out[step] = part(3).astype(jnp.bfloat16)
-
-    def relay(step):
-        first_copy(step).wait_recv()
-        for start in range(0, held, PAD):
-            rows = slice(start, start + PAD)
-            total = middle[step, rows] + first_in[step, rows].astype(jnp.float32)
-            along_out[step, rows] = total.astype(jnp.bfloat16)
-        along_copy(step).start()
-        back_copy(step).start()
-
-    pl.semaphore_wait(barrier, 4)
-    meet(0)
-    each(0, LEAD, produce)
+    own_of = factor_rows(own_chunk, own_depth, vec)
+    mate_of = [
+        factor_rows(mate_chunk, mate_depth, (vec + 3 - 2 * side) % VECS) for side in range(2)
+    ]
+    for place, ahead in enumerate((1, 2, 0, 3)):
+        part = own_of((vec + ahead) % VECS)
+        own_factors[0, place * held : (place + 1) * held] = part
+        other = 3 - place if ahead % 2 else place
+        own_factors[1, other * held : (other + 1) * held] = part
+        for side in range(2):
+            owner = (vec + (ahead if side == 0 else VECS - ahead)) % VECS
+            mate_factors[side, place * held : (place + 1) * held] = mate_of[side](owner)
+
+    def inner(turn):
+        def run(side):
+            place = turn * 2 + side
+            step = inner_at(turn, side)
+            local_copy(step).wait()
+            for half in range(2):
+                raw_copy(turn, side, half).wait_recv()
+            tail_copy(turn, side).wait_recv()
+            own = stack_own(step)
+            pieces = [
+                raw_in[place, :, chunk * width : (chunk + 1) * width] for chunk in range(CHUNKS)
+            ]
+            mate = jnp.concatenate([*pieces, tail_in[place]], axis=0)
+
+            def part(rows):
+                return jnp.dot(
+                    own_factors[side, rows], own, preferred_element_type=jnp.float32
+                ) + jnp.dot(
+                    mate_factors[side, rows, : CHUNKS * (whole + 1)],
+                    mate,
+                    preferred_element_type=jnp.float32,
+                )
+
+            mid_out[place] = part(slice(0, 2 * held)).astype(jnp.bfloat16)
+            mid_copy(turn, side).start()
+            keep[place] = part(slice(2 * held, 4 * held))
+
+        each(0, 2, run)
 
     for copy in inputs:
         copy.wait()
@@ -318,19 +396,45 @@
             piece = moved[chunk * PAD : (chunk + 1) * PAD].astype(jnp.bfloat16)
             out[:, pl.ds(start, width)] = piece[:vector_part]
 
-    def finish(step):
-        plane = plane_at(step)
-        along_copy(step).wait_recv()
-        back_copy(step).wait_recv()
-        for start in range(0, held, PAD):
-            rows = slice(start, start + PAD)
-            total = values[plane + 1, rows] + along_in[step, rows].astype(jnp.float32)
-            total = total + back_in[step, rows].astype(jnp.float32)
-            rounded = total.astype(jnp.bfloat16)
-            exact = rounded.astype(jnp.float32)
-            values[plane + 1, rows] = exact
-            packed[step, rows] = rounded
-            stat_out[rows] += fold(exact * exact)
+    def settle(step, rows, rounded):
+        exact = rounded.astype(jnp.float32)
+        values[plane_at(step) + 1, rows] = exact
+        packed[step, rows] = rounded
+        stat_out[rows] += fold(exact * exact)
+
+    def join(turn):
+        def run(side):
+            place = turn * 2 + side
+            mid_copy(turn, 1 - side).wait_recv()
+
+            def total(start):
+                rows = slice(start, start + PAD)
+                return (keep[place, rows] + mid_in[place, rows].astype(jnp.float32)).astype(
+                    jnp.bfloat16
+                )
+
+            for start in range(0, held, PAD):
+                last_out[place, start : start + PAD] = total(held + start)
+            last_copy(turn, side).start()
+            step = inner_at(turn, side)
+            for start in range(0, held, PAD):
+                settle(step, slice(start, start + PAD), total(start))
+            write_eig(step)
+
+        each(0, 2, run)
+
+    def close(turn, is_last):
+        def run(side):
+            place = turn * 2 + side
+            last_copy(turn, side).wait_recv()
+            step = outer_at(turn, side)
+            for start in range(0, held, PAD):
+                rows = slice(start, start + PAD)
+                settle(step, rows, last_in[place, rows])
+            if not is_last:
+                write_eig(step)
+
+        each(0, 2, run)
 
     def write_eig(step):
         write(eig_out, plane_at(step), packed[step])
@@ -391,6 +495,13 @@
 
     sides = ((0, links_in, 0, 1), (1, links, 1, 0))
 
+    def make_hot(step):
+        start = pl.multiple_of(step * BLOCK, BLOCK)
+        for which, lists, *ends in sides:
+            for end, end_row in enumerate(ends):
+                cell = lists[:, pl.ds(end_row * slots + start, BLOCK)]
+                hot[2 * which + end, step] = ones_where(low_iota == (cell & (LANES - 1)))
+
     def link_block(step):
         start = pl.multiple_of(step * BLOCK, BLOCK)
         targets, picked, got = [], [], []
@@ -401,8 +512,7 @@
             )
             source = lists[:, pl.ds(source_row * slots + start, BLOCK)]
             targets.append(lists[:, pl.ds(target_row * slots + start, BLOCK)])
-            low = ones_where(low_iota == (source & (LANES - 1)))
-            rows = jnp.dot(stacked, low, preferred_element_type=jnp.float32)
+            rows = jnp.dot(stacked, hot[2 * which, step], preferred_element_type=jnp.float32)
             picked.append((source, rows))
         for source, rows in picked:
             high = jnp.broadcast_to(source >> 7, (held, BLOCK))
@@ -424,69 +534,67 @@
                 ],
                 axis=0,
             )
-            low = ones_where(low_iota == (target & (LANES - 1)))
             link_sums[which] += lax.dot_general(
-                placed, low, (((1,), (1,)), ((), ())), preferred_element_type=jnp.float32
+                placed,
+                hot[2 * which + 1, step],
+                (((1,), (1,)), ((), ())),
+                preferred_element_type=jnp.float32,
             )
 
     rounds = meet_sem.shape[0]
 
-    def advance(step):
-        for round_ in range(rounds):
-
-            @pl.when(step == 2 * round_ + 1)
-            def _():
-                pl.semaphore_wait(meet_sem.at[round_], 2)
-                if round_ + 1 < rounds:
-                    meet(round_ + 1)
-
-        @pl.when(step + LEAD < planes)
-        def _():
-            produce(step + LEAD)
-
-        @pl.when(step < planes)
-        def _():
-            relay(step)
-
-        @pl.when(step >= LAG)
-        def _():
-            finish(step - LAG)
-
-            write_eig(step - LAG)
-
-            @pl.when(step == LAG)
-            def _():
-                face_copy(0).start()
-
-            @pl.when(step == LAG + 1)
-            def _():
-                face_copy(1).start()
-
-        @pl.when(step >= LAG + 3)
-        def _():
-            stencil(step - LAG - 2, None)
-            write_res(step - LAG - 2, 0)
-
-        @pl.when(step == LINKS_AT)
-        def _():
-            face_copy(0).wait_recv()
-            face_copy(1).wait_recv()
-            links_copy().wait_recv()
-
-        @pl.when((step >= LINKS_AT) & (step < LINKS_AT + slots // BLOCK))
-        def _():
-            link_block(step - LINKS_AT)
-
-        @pl.when(step == LINKS_AT + slots // BLOCK)
-        def _():
-            stencil(0, 0)
-            write_res(0, 0)
-
-    last = planes - 1
-    each(0, last + LAG, advance)
-    finish(last)
-    for slot in range(3):
-        stencil(last - 2 + slot, 1 if slot == 2 else None, slot)
+    def met(round_):
+        pl.semaphore_wait(meet_sem.at[round_], 2)
+        if round_ + 1 < rounds:
+            meet(round_ + 1)
+
+    def plain(plane):
+        stencil(plane, None)
+        write_res(plane, 0)
+
+    blocks = slots // BLOCK
+
+    inner(0)
+    send_half(2, 0)
+    met(0)
+    links_copy().wait_recv()
+    each(0, blocks, make_hot)
+    join(0)
+    send_half(2, 1)
+    send_tail(2)
+    inner(1)
+    met(1)
+    close(0, False)
+    face_copy(0).start()
+    face_copy(1).start()
+    send_half(3, 0)
+    plain(1)
+    met(2)
+    face_copy(0).wait_recv()
+    face_copy(1).wait_recv()
+    each(0, 2, link_block)
+    join(1)
+    send_half(3, 1)
+    send_tail(3)
+    inner(2)
+    each(2, 3, link_block)
+    met(3)
+    close(1, False)
+    each(2, 6, plain)
+    each(3, 4, link_block)
+    inner(3)
+    each(4, 6, link_block)
+    join(2)
+    each(6, blocks, link_block)
+    stencil(0, 0)
+    write_res(0, 0)
+    join(3)
+    close(2, False)
+    each(6, 10, plain)
+    close(3, True)
+    tail = range(10, planes)
+    for slot, plane in enumerate(tail):
+        stencil(plane, 1 if plane == planes - 1 else None, slot)
 
     sums = jnp.sum(stat_out[...].reshape(2 * vector_part, CHUNKS, LANES), axis=1)
     sums = jnp.sum(sums, axis=1, keepdims=True)
@@ -494,16 +602,19 @@
     line = jnp.sum(jnp.where(spot, sums, 0.0), axis=0, keepdims=True)
     stat_line[...] = line
     each(0, count - 1, lambda step: stat_copy(1 + (step + 11) % (count - 1)).start())
-    write_eig(last)
-    for slot in range(3):
-        write_res(last - 2 + slot, slot)
-
-    def sent(step):
-        first_copy(step).wait_send()
-        along_copy(step).wait_send()
-        back_copy(step).wait_send()
-
-    each(0, planes, sent)
+    each(0, 2, lambda side: write_eig(outer_at(turns - 1, side)))
+    for slot, plane in enumerate(tail):
+        write_res(plane, slot)
+
+    def sent(turn):
+        for side in range(2):
+            for half in range(2):
+                raw_copy(turn, side, half).wait_send()
+            tail_copy(turn, side).wait_send()
+            mid_copy(turn, side).wait_send()
+            last_copy(turn, side).wait_send()
+
+    each(0, turns, sent)
     links_copy().wait_send()
     face_copy(0).wait_send()
     face_copy(1).wait_send()
@@ -551,7 +662,12 @@
     vmem = pl.BlockSpec(memory_space=pltpu.VMEM)
     anywhere = pl.BlockSpec(memory_space=pltpu.HBM)
     dma = pltpu.SemaphoreType.DMA
-    wire = pltpu.VMEM((planes, held, width), jnp.bfloat16)
+    pairs = planes // VECS * 2
+    whole = rank_part // CHUNKS * CHUNKS
+
+    def wire(*shape):
+        return pltpu.VMEM(shape, jnp.bfloat16)
+
     eigvecs, residuals, norms = pl.pallas_call(
         functools.partial(kernel, count, planes, cells, vector_part, rank_part),
         out_shape=(
@@ -563,24 +679,27 @@
         out_specs=(vmem, vmem, vmem),
         scratch_shapes=[
             pltpu.VMEM((planes, rank_part, cells), jnp.bfloat16),
-            wire,
-            wire,
-            wire,
-            wire,
-            wire,
-            wire,
-            pltpu.VMEM((planes, held, width), jnp.float32),
+            wire(pairs, CHUNKS, width),
+            wire(pairs, whole, cells),
+            wire(pairs, CHUNKS, width),
+            wire(pairs, 2 * held, width),
+            wire(pairs, 2 * held, width),
+            pltpu.VMEM((pairs, 2 * held, width), jnp.float32),
+            wire(pairs, held, width),
+            wire(pairs, held, width),
             pltpu.VMEM((planes + 2, held, width), jnp.float32),
-            wire,
-            pltpu.VMEM((3, held, width), jnp.bfloat16),
+            wire(planes, held, width),
+            wire(6, held, width),
             pltpu.VMEM((2, held, width), jnp.bfloat16),
             pltpu.VMEM((1, 2 * slots), jnp.int32),
             pltpu.VMEM((1, 2 * slots), jnp.int32),
+            wire(4, slots // BLOCK, LANES, BLOCK),
             pltpu.VMEM((2, width // LANES * held, LANES), jnp.float32),
             pltpu.VMEM((2 * held, LANES), jnp.float32),
             pltpu.VMEM((count, 1, LANES), jnp.float32),
             pltpu.VMEM((1, LANES), jnp.float32),
-            pltpu.VMEM((2, 4 * held, CHUNKS * DEPTH), jnp.bfloat16),
+            wire(2, 4 * held, CHUNKS * DEPTH),
+            wire(2, 4 * held, CHUNKS * DEPTH),
             pltpu.VMEM((CHUNKS * PAD, held), jnp.bfloat16),
             pltpu.VMEM((held, held), jnp.bfloat16),
             pltpu.VMEM((3, held, LANES), jnp.float32),
@@ -594,12 +713,12 @@
             pltpu.VMEM((1, slots), jnp.int32),
             dma((8,)),
             dma((planes,)),
-            dma((planes,)),
-            dma((planes,)),
-            dma((planes,)),
-            dma((planes,)),
-            dma((planes,)),
-            dma((planes,)),
+            dma((3, pairs)),
+            dma((3, pairs)),
+            dma((pairs,)),
+            dma((pairs,)),
+            dma((pairs,)),
+            dma((pairs,)),
             dma((3,)),
             dma((3,)),
             dma((count,)),

time: 64.5 us -> 62.7 us (0.972)
  Pallas kernels: 63.1 us -> 61.3 us
    pallas_call x1, Pallas kernels: 61.1 us -> 59.2 us  [on_device(): pl.pallas_call(functools.partial(kernel, count, planes, cells, vector_par...]
where the time goes in v3:
time: 62.7 us; the launch traced here: 62.6 us
  Pallas kernels  61.3 us (98%)
  between operations  1.29 us (2%)
    pallas_call x1, Pallas kernels, on_device(): pl.pallas_call(functools.partial(kernel, count, planes, cells, vector_par...  59.2 us
    pallas_call x1, Pallas kernels, on_device(): pl.pallas_call(write_back, out_shape=tuple((jax.ShapeDtypeStruct(held.sha...  2.04 us

profile of v3, /device:TPU:1, one launch (start us, length us, event | category | flops | bytes accessed | tf_op | source)
XLA Modules:
  0.0 62.6 jit_solution(13462469263401752044)
XLA Ops:
  1.3 59.2 %shard_map.112 = (bf16[10,65536]{1,0:T(8,128)(2,1)S(1)}, bf16[10,65536]{1,0:T(8,128)(2,1)S(1)}, f32[1,10]{1,0:T(1,128)S(1)}) custom-call(bf16[25,65536]{1,0:T(8,128)(2,1)} %basis.1, bf16[40,100]{1,0:T(8,128)(2,1)} %bitcast.11, f32[1,10]{1,0:T(1,128)} %bitcast.12, f32[512,128]{1,0:T(8,128)} %bitcast.8, f32[512,128]{1,0:T(8,128)} %bitcast.9, ...), custom_call_target="tpu_custom_call" | custom-call | tf_op jit(solution)/shard_map/pallas_call | solution.py:671
  60.5 2.0 %shard_map.113 = (bf16[10,65536]{1,0:T(8,128)(2,1)}, bf16[10,65536]{1,0:T(8,128)(2,1)}, f32[1,10]{1,0:T(1,128)}) custom-call(bf16[10,65536]{1,0:T(8,128)(2,1)S(1)} %get-tuple-element.9.eig_held, bf16[10,65536]{1,0:T(8,128)(2,1)S(1)} %get-tuple-element.10.res_held, f32[1,10]{1,0:T(1,128)S(1)} %get-tuple-element.11.norm_held), custom_call_target="tpu_custom_call" | custom-call | tf_op jit(solution)/shard_map/pallas_call | solution.py:742

commit v4 on v3

--- a/solution.py
+++ b/solution.py
@@ -111,6 +111,8 @@
     plane_rows = cells // LANES
     whole = rank_part // CHUNKS * CHUNKS
     turns = planes // VECS
+    first = held // 2 // PAD * PAD + PAD
+    cuts = ((0, first), (first, held - first))
 
     def plane_at(step):
         return (step + planes - 1) % planes
@@ -156,24 +158,26 @@
             inward(side),
         )
 
-    def mid_copy(turn, side):
+    def mid_copy(turn, side, half):
         place = turn * 2 + side
         other = turn * 2 + 1 - side
+        rows = pl.ds((1 - half) * held, held)
         return remote(
-            mid_out.at[place],
-            mid_in.at[other],
-            mid_send.at[place],
-            mid_recv.at[other],
+            mid_out.at[place, rows],
+            mid_in.at[other, rows],
+            mid_send.at[half, place],
+            mid_recv.at[half, other],
             inward(side),
         )
 
-    def last_copy(turn, side):
+    def last_copy(turn, side, half):
         place = turn * 2 + side
+        rows = pl.ds(*cuts[half])
         return remote(
-            last_out.at[place],
-            last_in.at[place],
-            last_send.at[place],
-            last_recv.at[place],
+            last_out.at[place, rows],
+            last_in.at[place, rows],
+            last_send.at[half, place],
+            last_recv.at[half, place],
             outward(side),
         )
 
@@ -193,22 +197,31 @@
         return remote(
             stat_line,
             stat_in.at[step],
-            stat_send.at[step],
-            stat_recv.at[step],
+            stat_send.at[0],
+            stat_recv.at[0],
             {"rows": (row + step) % count},
         )
 
-    def each(first, last, body):
+    def all_stats():
+        lines = stat_in.at[pl.ds(1, count - 1)]
+        return remote(lines, lines, stat_send.at[0], stat_recv.at[0], above)
+
+    def each(begin, end, body):
         def run(step, carry):
             body(step)
             return carry
 
-        lax.fori_loop(first, last, run, 0)
+        lax.fori_loop(begin, end, run, 0)
 
     barrier = pltpu.get_barrier_semaphore()
 
     def greet(where):
         pl.semaphore_signal(barrier, inc=1, device_id=where, device_id_type=pl.DeviceIdType.MESH)
+
+    greet({"vecs": (vec + 1) % VECS})
+    greet({"vecs": (vec + 3) % VECS})
+    greet(above)
+    greet(below)
 
     coefficients_copy = pltpu.make_async_copy(coefficients_in, coefficients, input_sem.at[0])
     coefficients_copy.start()
@@ -236,10 +249,6 @@
     ]
     for copy in inputs:
         copy.start()
-    greet({"vecs": (vec + 1) % VECS})
-    greet({"vecs": (vec + 3) % VECS})
-    greet(above)
-    greet(below)
 
     def meet(round_):
         for where in (row + 2**round_, row + count - 2**round_):
@@ -351,7 +360,8 @@
                 )
 
             mid_out[place] = part(slice(0, 2 * held)).astype(jnp.bfloat16)
-            mid_copy(turn, side).start()
+            mid_copy(turn, side, 0).start()
+            mid_copy(turn, side, 1).start()
             keep[place] = part(slice(2 * held, 4 * held))
 
         each(0, 2, run)
@@ -403,36 +413,43 @@
         stat_out[rows] += fold(exact * exact)
 
     def join(turn):
-        def run(side):
+        def total(place, start):
+            rows = slice(start, start + PAD)
+            return (keep[place, rows] + mid_in[place, rows].astype(jnp.float32)).astype(
+                jnp.bfloat16
+            )
+
+        def send(side):
             place = turn * 2 + side
-            mid_copy(turn, 1 - side).wait_recv()
-
-            def total(start):
-                rows = slice(start, start + PAD)
-                return (keep[place, rows] + mid_in[place, rows].astype(jnp.float32)).astype(
-                    jnp.bfloat16
-                )
-
-            for start in range(0, held, PAD):
-                last_out[place, start : start + PAD] = total(held + start)
-            last_copy(turn, side).start()
+            mid_copy(turn, 1 - side, 0).wait_recv()
+            for half, (start, size) in enumerate(cuts):
+                for at in range(start, start + size, PAD):
+                    last_out[place, at : at + PAD] = total(place, held + at)
+                last_copy(turn, side, half).start()
+
+        def own(side):
+            place = turn * 2 + side
+            mid_copy(turn, 1 - side, 1).wait_recv()
             step = inner_at(turn, side)
             for start in range(0, held, PAD):
-                settle(step, slice(start, start + PAD), total(start))
+                settle(step, slice(start, start + PAD), total(place, start))
             write_eig(step)
 
-        each(0, 2, run)
-
-    def close(turn, is_last):
+        each(0, 2, send)
+        each(0, 2, own)
+
+    def close_part(turn, side, half):
+        last_copy(turn, side, half).wait_recv()
+        start, size = cuts[half]
+        for at in range(start, start + size, PAD):
+            rows = slice(at, at + PAD)
+            settle(outer_at(turn, side), rows, last_in[turn * 2 + side, rows])
+
+    def close(turn):
         def run(side):
-            place = turn * 2 + side
-            last_copy(turn, side).wait_recv()
-            step = outer_at(turn, side)
-            for start in range(0, held, PAD):
-                rows = slice(start, start + PAD)
-                settle(step, rows, last_in[place, rows])
-            if not is_last:
-                write_eig(step)
+            close_part(turn, side, 0)
+            close_part(turn, side, 1)
+            write_eig(outer_at(turn, side))
 
         each(0, 2, run)
 
@@ -450,14 +467,14 @@
     not_first = chunk_of != 0
     not_last = chunk_of != CHUNKS - 1
 
-    def stencil(plane, link, slot=0):
+    def stencil(plane, link, slot=0, begin=0, size=held):
         diagonals = []
         for part in range(parts):
             at = pl.ds(plane * plane_rows + part, CHUNKS, stride=parts)
             diagonals.append(
                 [jnp.concatenate([array[at]] * 2, axis=0) for array in (mass, damping, stiffness)]
             )
-        for start in range(0, held, PAD):
+        for start in range(begin, begin + size, PAD):
             rows = slice(start, start + PAD)
             lam = lam_of[0, rows]
             lam_sq = lam_of[1, rows]
@@ -564,7 +581,7 @@
     send_tail(2)
     inner(1)
     met(1)
-    close(0, False)
+    close(0)
     face_copy(0).start()
     face_copy(1).start()
     send_half(3, 0)
@@ -579,7 +596,7 @@
     inner(2)
     each(2, 3, link_block)
     met(3)
-    close(1, False)
+    close(1)
     each(2, 6, plain)
     each(3, 4, link_block)
     inner(3)
@@ -589,19 +606,22 @@
     stencil(0, 0)
     write_res(0, 0)
     join(3)
-    close(2, False)
+    close(2)
     each(6, 10, plain)
-    close(3, True)
     tail = range(10, planes)
-    for slot, plane in enumerate(tail):
-        stencil(plane, 1 if plane == planes - 1 else None, slot)
+    for half in range(2):
+        each(0, 2, lambda side: close_part(3, side, half))
+        for slot, plane in enumerate(tail):
+            stencil(plane, 1 if plane == planes - 1 else None, slot, *cuts[half])
 
     sums = jnp.sum(stat_out[...].reshape(2 * vector_part, CHUNKS, LANES), axis=1)
     sums = jnp.sum(sums, axis=1, keepdims=True)
     spot = iota((2 * vector_part, LANES), 0) == iota((2 * vector_part, LANES), 1)
     line = jnp.sum(jnp.where(spot, sums, 0.0), axis=0, keepdims=True)
     stat_line[...] = line
-    each(0, count - 1, lambda step: stat_copy(1 + (step + 11) % (count - 1)).start())
+    far = count // 3
+    each(far, count, lambda step: stat_copy(step).start())
+    each(1, far, lambda step: stat_copy(step).start())
     each(0, 2, lambda side: write_eig(outer_at(turns - 1, side)))
     for slot, plane in enumerate(tail):
         write_res(plane, slot)
@@ -611,19 +631,20 @@
             for half in range(2):
                 raw_copy(turn, side, half).wait_send()
             tail_copy(turn, side).wait_send()
-            mid_copy(turn, side).wait_send()
-            last_copy(turn, side).wait_send()
+            for half in range(2):
+                mid_copy(turn, side, half).wait_send()
+                last_copy(turn, side, half).wait_send()
 
     each(0, turns, sent)
     links_copy().wait_send()
     face_copy(0).wait_send()
     face_copy(1).wait_send()
-    each(1, count, lambda step: stat_copy(step).wait_recv())
+    all_stats().wait_recv()
     for step in range(1, count):
         line = line + stat_in[step]
     norms = jnp.sqrt(line[:, vector_part : 2 * vector_part]) / jnp.sqrt(line[:, :vector_part] + 1.0)
     norm_out[...] = norms
-    each(1, count, lambda step: stat_copy(step).wait_send())
+    all_stats().wait_send()
 
 
 def write_back(eig_held, res_held, norm_held, eig_out, res_out, norm_out, sem):
@@ -715,14 +736,14 @@
             dma((planes,)),
             dma((3, pairs)),
             dma((3, pairs)),
-            dma((pairs,)),
-            dma((pairs,)),
-            dma((pairs,)),
-            dma((pairs,)),
+            dma((2, pairs)),
+            dma((2, pairs)),
+            dma((2, pairs)),
+            dma((2, pairs)),
             dma((3,)),
             dma((3,)),
-            dma((count,)),
-            dma((count,)),
+            dma((1,)),
+            dma((1,)),
             pltpu.SemaphoreType.REGULAR((rounds,)),
         ],
         compiler_params=pltpu.CompilerParams(

time: 62.7 us -> 59.6 us (0.951)
  Pallas kernels: 61.3 us -> 58.2 us
    pallas_call x1, Pallas kernels: 59.2 us -> 56.1 us  [on_device(): pl.pallas_call(functools.partial(kernel, count, planes, cells, vector_par...]
where the time goes in v4:
time: 59.6 us; the launch traced here: 59.5 us
  Pallas kernels  58.2 us (98%)
  between operations  1.29 us (2%)
    pallas_call x1, Pallas kernels, on_device(): pl.pallas_call(functools.partial(kernel, count, planes, cells, vector_par...  56.1 us
    pallas_call x1, Pallas kernels, on_device(): pl.pallas_call(write_back, out_shape=tuple((jax.ShapeDtypeStruct(held.sha...  2.04 us

profile of v4, /device:TPU:1, one launch (start us, length us, event | category | flops | bytes accessed | tf_op | source)
XLA Modules:
  0.0 59.5 jit_solution(3795283461343716374)
XLA Ops:
  1.3 56.1 %shard_map.112 = (bf16[10,65536]{1,0:T(8,128)(2,1)S(1)}, bf16[10,65536]{1,0:T(8,128)(2,1)S(1)}, f32[1,10]{1,0:T(1,128)S(1)}) custom-call(bf16[25,65536]{1,0:T(8,128)(2,1)} %basis.1, bf16[40,100]{1,0:T(8,128)(2,1)} %bitcast.11, f32[1,10]{1,0:T(1,128)} %bitcast.12, f32[512,128]{1,0:T(8,128)} %bitcast.8, f32[512,128]{1,0:T(8,128)} %bitcast.9, ...), custom_call_target="tpu_custom_call" | custom-call | tf_op jit(solution)/shard_map/pallas_call | solution.py:692
  57.4 2.0 %shard_map.113 = (bf16[10,65536]{1,0:T(8,128)(2,1)}, bf16[10,65536]{1,0:T(8,128)(2,1)}, f32[1,10]{1,0:T(1,128)}) custom-call(bf16[10,65536]{1,0:T(8,128)(2,1)S(1)} %get-tuple-element.9.eig_held, bf16[10,65536]{1,0:T(8,128)(2,1)S(1)} %get-tuple-element.10.res_held, f32[1,10]{1,0:T(1,128)S(1)} %get-tuple-element.11.norm_held), custom_call_target="tpu_custom_call" | custom-call | tf_op jit(solution)/shard_map/pallas_call | solution.py:763

commit v5 on v4

--- a/solution.py
+++ b/solution.py
@@ -202,6 +202,10 @@
             {"rows": (row + step) % count},
         )
 
+    def distance(step):
+        across, along = step // 8, step // 2 % 4
+        return -min(across, 4 - across) - min(along, 4 - along)
+
     def all_stats():
         lines = stat_in.at[pl.ds(1, count - 1)]
         return remote(lines, lines, stat_send.at[0], stat_recv.at[0], above)
@@ -412,7 +416,7 @@
         packed[step, rows] = rounded
         stat_out[rows] += fold(exact * exact)
 
-    def join(turn):
+    def join(turn, late=False):
         def total(place, start):
             rows = slice(start, start + PAD)
             return (keep[place, rows] + mid_in[place, rows].astype(jnp.float32)).astype(
@@ -433,7 +437,8 @@
             step = inner_at(turn, side)
             for start in range(0, held, PAD):
                 settle(step, slice(start, start + PAD), total(place, start))
-            write_eig(step)
+            if not late:
+                write_eig(step)
 
         each(0, 2, send)
         each(0, 2, own)
@@ -445,11 +450,12 @@
             rows = slice(at, at + PAD)
             settle(outer_at(turn, side), rows, last_in[turn * 2 + side, rows])
 
-    def close(turn):
+    def close(turn, late=False):
         def run(side):
             close_part(turn, side, 0)
             close_part(turn, side, 1)
-            write_eig(outer_at(turn, side))
+            if not late:
+                write_eig(outer_at(turn, side))
 
         each(0, 2, run)
 
@@ -598,33 +604,36 @@
     met(3)
     close(1)
     each(2, 6, plain)
-    each(3, 4, link_block)
+    each(3, 5, link_block)
     inner(3)
-    each(4, 6, link_block)
+    each(5, blocks, link_block)
     join(2)
-    each(6, blocks, link_block)
     stencil(0, 0)
     write_res(0, 0)
-    join(3)
-    close(2)
-    each(6, 10, plain)
+    join(3, True)
+    close(2, True)
+    late = 6
+    each(late, 10, lambda plane: stencil(plane, None, plane - late))
     tail = range(10, planes)
     for half in range(2):
         each(0, 2, lambda side: close_part(3, side, half))
-        for slot, plane in enumerate(tail):
-            stencil(plane, 1 if plane == planes - 1 else None, slot, *cuts[half])
+        for plane in tail:
+            stencil(plane, 1 if plane == planes - 1 else None, plane - late, *cuts[half])
 
     sums = jnp.sum(stat_out[...].reshape(2 * vector_part, CHUNKS, LANES), axis=1)
     sums = jnp.sum(sums, axis=1, keepdims=True)
     spot = iota((2 * vector_part, LANES), 0) == iota((2 * vector_part, LANES), 1)
     line = jnp.sum(jnp.where(spot, sums, 0.0), axis=0, keepdims=True)
     stat_line[...] = line
-    far = count // 3
-    each(far, count, lambda step: stat_copy(step).start())
-    each(1, far, lambda step: stat_copy(step).start())
-    each(0, 2, lambda side: write_eig(outer_at(turns - 1, side)))
-    for slot, plane in enumerate(tail):
-        write_res(plane, slot)
+    for step in sorted(range(1, count), key=distance):
+        stat_copy(step).start()
+    def write_late(side):
+        write_eig(outer_at(2, side))
+        write_eig(inner_at(3, side))
+        write_eig(outer_at(3, side))
+
+    each(0, 2, write_late)
+    each(late, planes, lambda plane: write_res(plane, plane - late))
 
     def sent(turn):
         for side in range(2):
@@ -710,7 +719,7 @@
             wire(pairs, held, width),
             pltpu.VMEM((planes + 2, held, width), jnp.float32),
             wire(planes, held, width),
-            wire(6, held, width),
+            wire(10, held, width),
             pltpu.VMEM((2, held, width), jnp.bfloat16),
             pltpu.VMEM((1, 2 * slots), jnp.int32),
             pltpu.VMEM((1, 2 * slots), jnp.int32),

time: 59.6 us -> 58.6 us (0.983)
  Pallas kernels: 58.2 us -> 57.2 us
    pallas_call x1, Pallas kernels: 56.1 us -> 55.2 us  [on_device(): pl.pallas_call(functools.partial(kernel, count, planes, cells, vector_par...]
where the time goes in v5:
time: 58.6 us; the launch traced here: 58.5 us
  Pallas kernels  57.2 us (98%)
  between operations  1.29 us (2%)
    pallas_call x1, Pallas kernels, on_device(): pl.pallas_call(functools.partial(kernel, count, planes, cells, vector_par...  55.2 us
    pallas_call x1, Pallas kernels, on_device(): pl.pallas_call(write_back, out_shape=tuple((jax.ShapeDtypeStruct(held.sha...  2.04 us

profile of v5, /device:TPU:1, one launch (start us, length us, event | category | flops | bytes accessed | tf_op | source)
XLA Modules:
  0.0 58.5 jit_solution(11390881720706756371)
XLA Ops:
  1.3 55.2 %shard_map.112 = (bf16[10,65536]{1,0:T(8,128)(2,1)S(1)}, bf16[10,65536]{1,0:T(8,128)(2,1)S(1)}, f32[1,10]{1,0:T(1,128)S(1)}) custom-call(bf16[25,65536]{1,0:T(8,128)(2,1)} %basis.1, bf16[40,100]{1,0:T(8,128)(2,1)} %bitcast.11, f32[1,10]{1,0:T(1,128)} %bitcast.12, f32[512,128]{1,0:T(8,128)} %bitcast.8, f32[512,128]{1,0:T(8,128)} %bitcast.9, ...), custom_call_target="tpu_custom_call" | custom-call | tf_op jit(solution)/shard_map/pallas_call | solution.py:701
  56.5 2.0 %shard_map.113 = (bf16[10,65536]{1,0:T(8,128)(2,1)}, bf16[10,65536]{1,0:T(8,128)(2,1)}, f32[1,10]{1,0:T(1,128)}) custom-call(bf16[10,65536]{1,0:T(8,128)(2,1)S(1)} %get-tuple-element.9.eig_held, bf16[10,65536]{1,0:T(8,128)(2,1)S(1)} %get-tuple-element.10.res_held, f32[1,10]{1,0:T(1,128)S(1)} %get-tuple-element.11.norm_held), custom_call_target="tpu_custom_call" | custom-call | tf_op jit(solution)/shard_map/pallas_call | solution.py:772

commit v6 on v5

--- a/solution.py
+++ b/solution.py
@@ -139,7 +139,8 @@
 
     def raw_copy(turn, side, half):
         place = turn * 2 + side
-        lanes = pl.ds(half * (cells // 2), cells // 2)
+        early = cells // 8 * 5
+        lanes = pl.ds(half * early, cells - early if half else early)
         return remote(
             own_basis.at[outer_at(turn, side), pl.ds(0, whole), lanes],
             raw_in.at[place, :, lanes],
@@ -616,7 +617,8 @@
     each(late, 10, lambda plane: stencil(plane, None, plane - late))
     tail = range(10, planes)
     for half in range(2):
-        each(0, 2, lambda side: close_part(3, side, half))
+        for side in range(2):
+            close_part(3, side, half)
         for plane in tail:
             stencil(plane, 1 if plane == planes - 1 else None, plane - late, *cuts[half])
 

time: 58.6 us -> 58.7 us (level)
  no operation moved by 1% of the time
where the time goes in v6:
time: 58.7 us; the launch traced here: 58.6 us
  Pallas kernels  57.3 us (98%)
  between operations  1.29 us (2%)
    pallas_call x1, Pallas kernels, on_device(): pl.pallas_call(functools.partial(kernel, count, planes, cells, vector_par...  55.2 us
    pallas_call x1, Pallas kernels, on_device(): pl.pallas_call(write_back, out_shape=tuple((jax.ShapeDtypeStruct(held.sha...  2.04 us

profile of v6, /device:TPU:1, one launch (start us, length us, event | category | flops | bytes accessed | tf_op | source)
XLA Modules:
  0.0 58.6 jit_solution(13353805285145163165)
XLA Ops:
  1.3 55.2 %shard_map.112 = (bf16[10,65536]{1,0:T(8,128)(2,1)S(1)}, bf16[10,65536]{1,0:T(8,128)(2,1)S(1)}, f32[1,10]{1,0:T(1,128)S(1)}) custom-call(bf16[25,65536]{1,0:T(8,128)(2,1)} %basis.1, bf16[40,100]{1,0:T(8,128)(2,1)} %bitcast.11, f32[1,10]{1,0:T(1,128)} %bitcast.12, f32[512,128]{1,0:T(8,128)} %bitcast.8, f32[512,128]{1,0:T(8,128)} %bitcast.9, ...), custom_call_target="tpu_custom_call" | custom-call | tf_op jit(solution)/shard_map/pallas_call | solution.py:703
  56.5 2.0 %shard_map.113 = (bf16[10,65536]{1,0:T(8,128)(2,1)}, bf16[10,65536]{1,0:T(8,128)(2,1)}, f32[1,10]{1,0:T(1,128)}) custom-call(bf16[10,65536]{1,0:T(8,128)(2,1)S(1)} %get-tuple-element.9.eig_held, bf16[10,65536]{1,0:T(8,128)(2,1)S(1)} %get-tuple-element.10.res_held, f32[1,10]{1,0:T(1,128)S(1)} %get-tuple-element.11.norm_held), custom_call_target="tpu_custom_call" | custom-call | tf_op jit(solution)/shard_map/pallas_call | solution.py:774
